TPU v7x, 32 devices: a whole 2x2x4 slice. The times are simulated.
32 devices in a mesh: pop: 8 (over z, x), mp: 4 (over y, core).
Axes of the slice: x: 2, y: 2, z: 4, core: 2. Of those that a mesh axis runs over, the one named last changes fastest.
Arguments:
- tokens: bfloat16 [256, 3584], replicated, may hold values from -60 to 60
- target: bfloat16 [256, 3584], P(None, 'mp'), may hold values from -6 to 6
- w_query: bfloat16 [3584, 3584], P('pop', 'mp'), may hold values from -0.09375 to 0.09375
- w_key: bfloat16 [3584, 512], P(None, 'mp'), may hold values from -0.09375 to 0.09375
- w_value: bfloat16 [3584, 512], P(None, 'mp'), may hold values from -0.09375 to 0.09375
- w_out: bfloat16 [3584, 3584], P('mp', 'pop'), may hold values from -0.09375 to 0.09375
- query_left_factors: bfloat16 [8, 3584, 4], P('pop'), may hold values from -0.09375 to 0.09375
- query_right_factors: bfloat16 [8, 4, 3584], P('pop', None, 'mp'), may hold values from -6 to 6
- o_left: bfloat16 [8, 3584, 4], P('pop', 'mp'), may hold values from -0.09375 to 0.09375
- o_right: bfloat16 [8, 4, 3584], P('pop'), may hold values from -6 to 6
- member_ids: int32 [8], P('pop'), may hold values from 0 to 7, each once
Outputs:
- grad_query: float32 [3584, 3584], P('pop', 'mp')
- grad_out: float32 [3584, 3584], P('mp', 'pop')
- fitness: float32 [8], P('pop')
Inputs may be any that keep to these rules, and one draw needn't show every extreme that they name: `member_ids`: every number from 0 to 7 appears once.
All inputs are finite; a program needn't handle non-finite values.
Results may differ from a plain program's by a relative error of at most 0.005.
Values may be sent and summed in bfloat16 or wider, within the bound.
A program may use at most 64 MiB of HBM per device.

v0:
```python
import math

import jax
import jax.numpy as jnp
from jax import lax
from jax.sharding import PartitionSpec as P

D = 3584
HEADS = 28
KV_HEADS = 4
HEAD_DIM = 128
RANK = 4


noise_scale = 0.5
rope_base = 1000000.0
spread_floor = 0.001


def tables(count, head_size):
    position = jnp.arange(count, dtype=jnp.float32)
    index = jnp.arange(head_size // 2, dtype=jnp.float32)
    freq = jnp.exp(-math.log(rope_base) * 2.0 * index / head_size)
    angle = position[:, None] * freq[None, :]
    return (jnp.cos(angle)[:, None, :], jnp.sin(angle)[:, None, :])


def rotate(field, cosine_table, sine):
    half = field.shape[-1] // 2
    first = field[..., :half]
    second = field[..., half:]
    return jnp.concatenate(
        [first * cosine_table - second * sine, second * cosine_table + first * sine], axis=-1
    )


def per_device(
    tokens,
    target,
    w_query,
    w_key,
    w_value,
    w_out,
    query_left_factors,
    query_right_factors,
    o_left,
    o_right,
    member_ids,
):
    tok = tokens.shape[0]
    local_feats = w_query.shape[1]
    local_kv = w_key.shape[1] // HEAD_DIM
    group = HEADS // KV_HEADS
    local_heads = local_kv * group
    slots = query_left_factors.shape[0]
    scale = HEAD_DIM ** (-0.5)
    cosine_table, sine = tables(tok, HEAD_DIM)
    base = jnp.dot(
        tokens,
        lax.all_gather(w_query, "pop", axis=0, tiled=True),
        preferred_element_type=jnp.float32,
    )
    keys = rotate(
        jnp.dot(tokens, w_key, preferred_element_type=jnp.float32).reshape(tok, local_kv, HEAD_DIM),
        cosine_table,
        sine,
    ).astype(jnp.bfloat16)
    values = (
        jnp.dot(tokens, w_value, preferred_element_type=jnp.float32)
        .astype(jnp.bfloat16)
        .reshape(tok, local_kv, HEAD_DIM)
    )
    signs = (1 - 2 * (member_ids % 2)).astype(jnp.float32)
    factor = noise_scale * signs[:, None, None]
    lowrank_product = jnp.einsum(
        "td,mdr->mtr", tokens, query_left_factors, preferred_element_type=jnp.float32
    ).astype(jnp.bfloat16)
    query = base[None] + factor * jnp.einsum(
        "olj,ojv->olv", lowrank_product, query_right_factors, preferred_element_type=jnp.float32
    )
    query = rotate(
        query.reshape(slots, tok, local_heads, HEAD_DIM), cosine_table[None], sine[None]
    ).astype(jnp.bfloat16)
    query = query.reshape(slots, tok, local_kv, group, HEAD_DIM)
    scores = jnp.einsum("mtkgd,skd->mkgts", query, keys, preferred_element_type=jnp.float32) * scale
    causal = jnp.arange(tok)[:, None] >= jnp.arange(tok)[None, :]
    scores = jnp.where(causal, scores, -1e30)
    probs = jax.nn.softmax(scores, axis=-1).astype(jnp.bfloat16)
    mixed = (
        jnp.einsum("mkgts,skd->mtkgd", probs, values, preferred_element_type=jnp.float32)
        .astype(jnp.bfloat16)
        .reshape(slots, tok, local_feats)
    )
    low_out = jnp.einsum("mtf,mfr->mtr", mixed, o_left, preferred_element_type=jnp.float32)
    right_full = o_right.astype(jnp.float32)
    part = jnp.einsum(
        "mtf,fe->mte",
        mixed,
        lax.all_gather(w_out, "pop", axis=1, tiled=True),
        preferred_element_type=jnp.float32,
    )
    term = part + factor * jnp.einsum(
        "mtr,mre->mte", low_out, right_full, precision=lax.Precision.HIGHEST
    )
    output = lax.psum_scatter(
        term.astype(jnp.bfloat16), "mp", scatter_dimension=2, tiled=True
    ).astype(jnp.float32)
    diff = output - target.astype(jnp.float32)[None]
    errors = lax.psum(jnp.sum(diff * diff, axis=(1, 2)), "mp")
    fitness = -(errors / (tok * D))
    count = slots * lax.axis_size("pop")
    mean = lax.psum(jnp.sum(fitness), "pop") / count
    spread = lax.psum(jnp.sum((fitness - mean) * (fitness - mean)), "pop") / count
    weight = signs * (fitness - mean) / jnp.sqrt(spread + spread_floor)
    every_weight = lax.all_gather(weight, "pop", axis=0, tiled=True)
    right_factors_gathered, left_all = (
        lax.all_gather(query_right_factors, "pop", axis=0, tiled=True),
        lax.all_gather(o_left, "pop", axis=0, tiled=True),
    )
    rows_q = lax.all_to_all(query_left_factors, "pop", split_axis=1, concat_axis=0, tiled=True)
    cols_o = lax.all_to_all(o_right, "pop", split_axis=2, concat_axis=0, tiled=True)
    whole_population = rows_q.shape[0]
    left_q = jnp.transpose(
        rows_q.astype(jnp.float32) * every_weight[:, None, None], (1, 0, 2)
    ).reshape(rows_q.shape[1], whole_population * RANK)
    right_q = right_factors_gathered.astype(jnp.float32).reshape(
        whole_population * RANK, local_feats
    )
    grad_query = jnp.dot(left_q, right_q, precision=lax.Precision.HIGHEST) / noise_scale
    output_left_factor = jnp.transpose(
        left_all.astype(jnp.float32) * every_weight[:, None, None], (1, 0, 2)
    ).reshape(local_feats, whole_population * RANK)
    right_o = cols_o.astype(jnp.float32).reshape(whole_population * RANK, cols_o.shape[2])
    grad_out = jnp.dot(output_left_factor, right_o, precision=lax.Precision.HIGHEST) / noise_scale
    return (grad_query, grad_out, fitness)


def solution(mesh):
    placed = (
        P(),
        P(None, "mp"),
        P("pop", "mp"),
        P(None, "mp"),
        P(None, "mp"),
        P("mp", "pop"),
        P("pop", None, None),
        P("pop", None, "mp"),
        P("pop", "mp", None),
        P("pop", None, None),
        P("pop"),
    )
    return jax.shard_map(
        per_device,
        mesh=mesh,
        in_specs=placed,
        out_specs=(P("pop", "mp"), P("mp", "pop"), P("pop")),
        check_vma=False,
    )
```

profile of v0, /device:TPU:0, one launch (start us, length us, event | category | flops | bytes accessed | tf_op | source)
XLA Modules:
  0.0 465.0 jit_solution(14919115663158646740)
XLA Ops:
  7.2 0.7 all-gather.3.cloned.1.call-update
  8.0 0.7 all-gather.5.cloned.1.call-update
  9.4 0.6 fusion.35
  10.0 0.7 convolution_bitcast_fusion
  10.8 1.0 fusion.25
  12.2 101.0 %all-gather.3.cloned.1.call-done = bf16[3584,896]{1,0:T(8,128)(2,1)} async-done(((bf16[448,896]{1,0:T(8,128)(2,1)}), bf16[3584,896]{1,0:T(8,128)(2,1)}) %all-gather.3.cloned.1.call-update) | async-done | bytes 6422544 | tf_op jit(solution)/shard_map/all_gather | solution.py:60
  113.2 4.9 %fusion.37 = f32[256,896]{1,0:T(8,128)S(1)} fusion(bf16[256,3584]{1,0:T(8,128)(2,1)S(1)} %copy-done, bf16[3584,896]{1,0:T(8,128)(2,1)} %all-gather.3.cloned.1.call-done), kind=kOutput, calls=%fused_computation.66 | convolution fusion | flops 1644167168 | bytes 9175040 | tf_op jit(solution)/shard_map/dot_general | solution.py:58
  118.1 2.7 fusion.4
  120.8 1.6 copy.38
  122.4 0.9 fusion.34
  123.3 1.3 copy.57
  124.6 1.2 copy.58
  125.9 1.4 fusion.10
  127.3 0.6 fusion.36
  127.9 1.2 copy-done.1
  129.5 2.9 convolution_convert_fusion
  132.5 81.4 %all-gather.5.cloned.1.call-done = bf16[896,3584]{0,1:T(8,128)(2,1)} async-done(((bf16[896,448]{0,1:T(8,128)(2,1)}), bf16[896,3584]{0,1:T(8,128)(2,1)}) %all-gather.5.cloned.1.call-update) | async-done | bytes 6422544 | tf_op jit(solution)/shard_map/all_gather | solution.py:99
  213.9 4.9 %fusion.38 = f32[256,3584]{1,0:T(8,128)S(1)} fusion(bf16[256,896]{0,1:T(8,128)(2,1)S(1)} %bitcast.110, bf16[896,3584]{0,1:T(8,128)(2,1)} %all-gather.5.cloned.1.call-done), kind=kOutput, calls=%fused_computation.67 | convolution fusion | flops 1644167168 | bytes 10551296 | tf_op jit(solution)/shard_map/mtf,fe->mte/dot_general | solution.py:96
  218.9 3.7 fusion.2
  222.6 8.8 %copy.54 = bf16[1,256,3584]{1,0,2:T(2,128)(2,1)} copy(bf16[1,256,3584]{2,1,0:T(8,128)(2,1)} %fusion.2) | data formatting | bytes 3670016
  231.4 3.6 copy.62
  235.0 3.2 copy.46
  238.3 0.5 broadcast.87
  238.8 20.8 %reduce.4 = bf16[3584,4]{1,0:T(8,128)(2,1)S(1)} reduce(bf16[3584,1,4]{2,1,0:T(2,128)(2,1)} %bitcast.105, bf16[]{:T(256)} %broadcast.87), dimensions={1}, to_apply=%bitcast.83.reduce_sub_computation | reduce | bytes 57346
  259.6 2.2 reshape.258
  261.8 3.6 all-to-all-start.1
  265.4 3.2 copy.37
  268.6 20.7 %reduce.3 = bf16[3584,4]{1,0:T(8,128)(2,1)S(1)} reduce(bf16[3584,1,4]{2,1,0:T(2,128)(2,1)} %bitcast.106, bf16[]{:T(256)} %broadcast.87), dimensions={1}, to_apply=%bitcast.81.reduce_sub_computation | reduce | bytes 57346
  289.3 2.2 reshape.256
  291.6 0.6 dynamic-slice
  292.2 5.7 %all-to-all-start = ((bf16[8,2,896]{2,1,0:T(2,128)(2,1)}), bf16[8,2,896]{2,1,0:T(2,128)(2,1)S(1)}, u32[]{:S(2)}, u32[]{:S(2)}) async-start(bf16[8,2,896]{2,1,0:T(2,128)(2,1)} %reshape.256), calls=%async_computation | async-start | bytes 57344 | tf_op jit(solution)/shard_map/all_to_all | solution.py:120
  297.8 31.3 %all_gather.19 = bf16[8,896,4]{1,2,0:T(4,128)(2,1)S(1)} all-gather(bf16[1,896,4]{1,2,0:T(4,128)(2,1)S(1)} %copy-done.8), channel_id=1, replica_groups=mesh['pop'=8,'mp'=4] {'pop'}, dimensions={0}, use_global_device_ids=true | all-gather | bytes 64512 | tf_op jit(solution)/shard_map/all_gather | solution.py:118
  329.1 30.7 %all_gather.18 = bf16[8,4,896]{2,1,0:T(4,128)(2,1)S(1)} all-gather(bf16[1,4,896]{2,1,0:T(4,128)(2,1)S(1)} %copy-done.9), channel_id=1, replica_groups=mesh['pop'=8,'mp'=4] {'pop'}, dimensions={0}, use_global_device_ids=true | all-gather | bytes 64512 | tf_op jit(solution)/shard_map/all_gather | solution.py:117
  359.8 3.3 reshape.259
  363.2 3.6 copy.47
  367.0 3.3 reshape.257
  370.3 4.6 bitcast_convert_fusion
  374.9 1.5 reshape_bitcast_fusion
  376.4 1.6 copy.55
  378.0 1.9 fusion.8
  379.8 6.3 %psum.21 = f32[1]{0:T(128)} all-reduce(f32[1]{0:T(128)} %bitcast.27), channel_id=1, replica_groups=mesh['pop'=8,'mp'=4] {'mp'}, use_global_device_ids=true, to_apply=%region_4.5 | all-reduce | flops 1 | bytes 8 | tf_op jit(solution)/shard_map/psum | solution.py:109
  387.2 21.8 %psum.22 = f32[]{:T(128)} all-reduce(f32[]{:T(128)} %bitcast.28), channel_id=1, replica_groups=mesh['pop'=8,'mp'=4] {'pop'}, use_global_device_ids=true, to_apply=%region_5.6 | all-reduce | flops 1 | bytes 8 | tf_op jit(solution)/shard_map/psum | solution.py:112
  412.1 18.3 %psum.23 = f32[]{:T(128)} all-reduce(f32[]{:T(128)} %bitcast.30), channel_id=1, replica_groups=mesh['pop'=8,'mp'=4] {'pop'}, use_global_device_ids=true, to_apply=%region_6.7 | all-reduce | flops 1 | bytes 8 | tf_op jit(solution)/shard_map/psum | solution.py:113
  431.1 1.9 divide_dynamic-update-slice_fusion
  433.0 2.1 copy.44
  435.2 19.1 %all-reduce = f32[8]{0:T(128)S(1)} all-reduce(f32[8]{0:T(128)S(1)} %divide_dynamic-update-slice_fusion), channel_id=1, replica_groups=mesh['pop'=8,'mp'=4] {'pop'}, use_global_device_ids=true, to_apply=%add | all-reduce | flops 8 | bytes 64
  454.4 2.0 convolution_multiply_fusion.1
  456.4 2.1 bitcast_multiply_fusion
  (39 shorter events, 1.4 us)
Async XLA Ops:
  7.2 2.8 copy-start
  7.2 2.8 copy-start.2
  7.2 106.0 %all-gather.3.cloned.1.call-start = ((), (), s32[]{:S(2)}) async-start(), calls=%async_computation.3 | async-start | bytes 7225344 | tf_op jit(solution)/shard_map/all_gather | solution.py:60
  7.9 206.0 %all-gather.5.cloned.1.call-start = ((), (), s32[]{:S(2)}) async-start(), calls=%async_computation.4 | async-start | bytes 7225344 | tf_op jit(solution)/shard_map/all_gather | solution.py:99
  8.7 366.2 %reduce-scatter.4.cloned.1.call-start = ((), (), s32[]{:S(2)}) async-start(), calls=%async_computation.5 | async-start | bytes 2293760
  12.2 105.9 %copy-start.6 = (bf16[1,3584,4]{1,2,0:T(4,128)(2,1)S(1)}, bf16[1,3584,4]{1,2,0:T(4,128)(2,1)}, u32[]{:S(2)}) copy-start(bf16[1,3584,4]{1,2,0:T(4,128)(2,1)} %param.17) | copy-start | bytes 86020
  12.2 105.9 %copy-start.9 = (bf16[1,4,896]{2,1,0:T(4,128)(2,1)S(1)}, bf16[1,4,896]{2,1,0:T(4,128)(2,1)}, u32[]{:S(2)}) copy-start(bf16[1,4,896]{2,1,0:T(4,128)(2,1)} %param.18) | copy-start | bytes 21508
  125.9 1.4 copy-start.3
  125.9 1.4 copy-start.4
  127.9 1.2 copy-start.1
  129.4 2.9 copy-start.8
  132.5 86.4 %copy-start.5 = (bf16[1,4,3584]{2,1,0:T(4,128)(2,1)S(1)}, bf16[1,4,3584]{2,1,0:T(4,128)(2,1)}, u32[]{:S(2)}) copy-start(bf16[1,4,3584]{2,1,0:T(4,128)(2,1)} %param.20) | copy-start | bytes 86020
  238.8 26.6 %copy-start.7 = (bf16[1,3584,4]{1,2,0:T(4,128)(2,1)S(1)}, bf16[1,3584,4]{1,2,0:T(4,128)(2,1)}, u32[]{:S(2)}) copy-start(bf16[1,3584,4]{1,2,0:T(4,128)(2,1)} %param.17) | copy-start | bytes 86020
  261.8 30.4 %all-to-all-start.1 = ((bf16[8,2,896]{2,1,0:T(2,128)(2,1)}), bf16[8,2,896]{2,1,0:T(2,128)(2,1)S(1)}, u32[]{:S(2)}, u32[]{:S(2)}) async-start(bf16[8,2,896]{2,1,0:T(2,128)(2,1)} %reshape.258), calls=%async_computation.1 | async-start | bytes 57344 | tf_op jit(solution)/shard_map/all_to_all | solution.py:121
  268.6 23.0 %copy-start.10 = (u32[32]{0:T(128)S(1)}, u32[32]{0:T(128)}, u32[]{:S(2)}) copy-start(u32[32]{0:T(128)} %constant.59) | copy-start | bytes 388
  292.2 74.8 %all-to-all-start = ((bf16[8,2,896]{2,1,0:T(2,128)(2,1)}), bf16[8,2,896]{2,1,0:T(2,128)(2,1)S(1)}, u32[]{:S(2)}, u32[]{:S(2)}) async-start(bf16[8,2,896]{2,1,0:T(2,128)(2,1)} %reshape.256), calls=%async_computation | async-start | bytes 57344 | tf_op jit(solution)/shard_map/all_to_all | solution.py:120
Sparse Core Ops, SparseCore 0:
  10.2 103.0 all-gather.2
  115.4 98.4 all-gather.4
  235.2 27.7 reduce-scatter.3
where the time goes:
time: 466 us; the launch traced here: 465 us
  waiting for transfers between devices  184 us (39%)
  blocking collectives  127 us (27%)
  other arithmetic  53.7 us (12%)
  local copies, waits for them, and re-layouts  46.4 us (10%)
  matrix products  24.7 us (5%)
  between operations  19.6 us (4%)
  starting transfers between devices  9.34 us (2%)
    all_gather x1, waiting for transfers between devices, per_device(): lax.all_gather(w_query, 'pop', axis=0, tiled=True)  101 us
    all_gather x1, waiting for transfers between devices, per_device(): lax.all_gather(w_out, 'pop', axis=1, tiled=True)  81.4 us
    unnamed x3, other arithmetic  43.4 us
    unnamed x37, local copies, waits for them, and re-layouts  38 us
    all_gather x1, blocking collectives, per_device(): lax.all_gather(o_left, 'pop', axis=0, tiled=True)  31.3 us
    all_gather x1, blocking collectives, per_device(): lax.all_gather(query_right_factors, 'pop', axis=0, tiled=True)  30.7 us
    psum x1, blocking collectives, per_device(): mean = lax.psum(jnp.sum(fitness), 'pop') / count  21.8 us
    unnamed x1, blocking collectives  19.1 us
  transfers between devices with their start and end apart: 5, of which 2 were waited for; matrix products, arithmetic and copies ran while one was open for 19% of the time, Pallas kernels for 0%

commit v1 on v0

--- a/solution.py
+++ b/solution.py
@@ -1,20 +1,426 @@
+import functools
 import math
 
 import jax
 import jax.numpy as jnp
+import numpy as np
 from jax import lax
+from jax.experimental import pallas as pl
+from jax.experimental.pallas import tpu as pltpu
 from jax.sharding import PartitionSpec as P
 
-D = 3584
-HEADS = 28
-KV_HEADS = 4
 HEAD_DIM = 128
 RANK = 4
-
+PACK = 16
+LINK = jnp.float32
 
 noise_scale = 0.5
 rope_base = 1000000.0
 spread_floor = 0.001
+MESH = pl.DeviceIdType.MESH
+f32 = jnp.float32
+bf16 = jnp.bfloat16
+
+
+def rope_tables(count, head_size):
+    index = np.arange(head_size // 2, dtype=np.float64)
+    freq = np.exp(-math.log(rope_base) * 2.0 * index / head_size)
+    angle = np.arange(count, dtype=np.float64)[:, None] * freq[None, :]
+    cosine, sine = np.cos(angle), np.sin(angle)
+    return (
+        np.concatenate([cosine, cosine], 1).astype(np.float32),
+        np.concatenate([-sine, sine], 1).astype(np.float32),
+    )
+
+
+def dot(a, b, dims=((1,), (0,))):
+    return lax.dot_general(a, b, (dims, ((), ())), preferred_element_type=f32)
+
+
+def split3(x):
+    hi = x.astype(bf16)
+    rest = x - hi.astype(f32)
+    mid = rest.astype(bf16)
+    low = (rest - mid.astype(f32)).astype(bf16)
+    return hi, mid, low
+
+
+def shift_half(pack):
+    rows = pack.shape[0]
+    row = lax.broadcasted_iota(jnp.int32, (rows, rows), 0)
+    col = lax.broadcasted_iota(jnp.int32, (rows, rows), 1)
+    perm = ((col == row + PACK // 2) & (row % PACK < PACK // 2)).astype(bf16)
+    return dot(perm, pack).astype(bf16)
+
+
+def forward_kernel(
+    n_pop, n_mp, width,
+    tok_ref, tokp_ref, wq_ref, wk_ref, wv_ref, wo_ref, qlt_ref, pkg_ref, tgt_ref, cos_ref, sin_ref,
+    pack_out, stat_out,
+    part, parts_in, lowq, lowq_in, packs, ring, terms, terms_in, target, errs, shifted,
+    base_send, base_recv, lowq_send, lowq_recv, pack_send, pack_recv,
+    ring_send, ring_recv, term_send, term_recv, tgt_send, tgt_recv, err_send, err_recv,
+):
+    me = lax.axis_index("pop")
+    mc = lax.axis_index("mp")
+    n_dev = n_pop * n_mp
+    tok, feats = part.shape[0] * part.shape[1], part.shape[2]
+    own_tok = tok // n_pop
+    rows = n_pop * own_tok
+    half = rows // 2
+    per_mp = rows // n_mp
+    heads = feats // HEAD_DIM
+    cols = wo_ref.shape[1]
+
+    barrier = pltpu.get_barrier_semaphore()
+
+    def greet(i, carry):
+        other = lax.rem(mc * n_pop + me + i, n_dev)
+        pl.semaphore_signal(
+            barrier, inc=1,
+            device_id={"pop": lax.rem(other, n_pop), "mp": other // n_pop},
+            device_id_type=MESH,
+        )
+        return carry
+
+    lax.fori_loop(1, n_dev, greet, 0)
+
+    part[...] = dot(tokp_ref[...], wq_ref[...]).reshape(part.shape).astype(part.dtype)
+    low = dot(tok_ref[...], qlt_ref[...], ((1,), (1,))).astype(bf16)
+    row = lax.broadcasted_iota(jnp.int32, (PACK, 128), 0)
+    lane = lax.broadcasted_iota(jnp.int32, (PACK, 128), 1)
+    spread_lanes = (lane == me * PACK + row).astype(bf16)
+    lowq[...] = dot(low, spread_lanes).astype(bf16).reshape(lowq.shape)
+    parts_in[me] = part[me]
+    lowq_in[me] = lowq[me]
+    packs[me] = pkg_ref[me]
+
+    pl.semaphore_wait(barrier, n_dev - 1)
+
+    def to_pop(i):
+        other = lax.rem(me + i, n_pop)
+        source = lax.rem(me + n_pop - i, n_pop)
+        out = []
+        for src, dst, send, recv in (
+            (part, parts_in, base_send, base_recv),
+            (lowq, lowq_in, lowq_send, lowq_recv),
+            (pkg_ref, packs, pack_send, pack_recv),
+        ):
+            out.append(
+                (
+                    pltpu.make_async_remote_copy(
+                        src_ref=src.at[other], dst_ref=dst.at[me], send_sem=send.at[i],
+                        recv_sem=recv.at[i], device_id={"pop": other}, device_id_type=MESH,
+                    )
+                )
+            )
+        return out
+
+    for i in range(1, n_pop):
+        for copy in to_pop(i):
+            copy.start()
+
+    owner = me // (n_pop // n_mp)
+
+    def target_copy(i):
+        return pltpu.make_async_remote_copy(
+            src_ref=tgt_ref, dst_ref=target, send_sem=tgt_send.at[i], recv_sem=tgt_recv,
+            device_id={"mp": lax.rem(mc + i, n_mp)}, device_id_type=MESH,
+        )
+
+    @pl.when(mc == owner)
+    def _():
+        for i in range(1, n_mp):
+            target_copy(i).start()
+        target[...] = tgt_ref[...]
+
+    cosine, sine = cos_ref[...], sin_ref[...]
+    key = dot(tok_ref[...], wk_ref[...])
+    key = (key * cosine + pltpu.roll(key, HEAD_DIM // 2, 1) * sine).astype(bf16)
+    value = dot(tok_ref[...], wv_ref[...]).astype(bf16)
+
+    for i in range(1, n_pop):
+        for copy in to_pop(i):
+            copy.wait_recv()
+
+    pack = packs[...].reshape(n_pop * PACK, feats)
+    shifted[...] = shift_half(pack[:, :cols]) if cols % 128 == 0 else shift_half(pack)[:, :cols]
+
+    def pop_at(r):
+        r = lax.rem(r + 2 * n_pop, n_pop)
+        return jnp.where(r < n_pop // 2, 2 * r, 2 * (n_pop - 1 - r) + 1)
+
+    my_r = jnp.where(lax.rem(me, 2) == 0, me // 2, n_pop - 1 - me // 2)
+    right, left = pop_at(my_r + 1), pop_at(my_r - 1)
+
+    total = parts_in[0].astype(f32)
+    for i in range(1, n_pop):
+        total = total + parts_in[i].astype(f32)
+    low_rows = lowq_in[...].reshape(rows, 128)
+    start = pl.multiple_of(me * own_tok, own_tok)
+    cos_own = jnp.tile(cos_ref[pl.ds(start, own_tok), :], (n_pop, 1))
+    sin_own = jnp.tile(sin_ref[pl.ds(start, own_tok), :], (n_pop, 1))
+    token_of = start + lax.rem(lax.broadcasted_iota(jnp.int32, (rows, tok), 0), own_tok)
+    causal = token_of >= lax.broadcasted_iota(jnp.int32, (rows, tok), 1)
+    scale = HEAD_DIM ** (-0.5)
+    for h in range(heads):
+        lanes = slice(h * HEAD_DIM, (h + 1) * HEAD_DIM)
+        q = jnp.tile(total[:, lanes], (n_pop, 1)) + dot(low_rows, pack[:, lanes])
+        q = (q * cos_own + pltpu.roll(q, HEAD_DIM // 2, 1) * sin_own).astype(bf16)
+        s = dot(q, key, ((1,), (1,))) * scale
+        s = jnp.where(causal, s, -1e30)
+        e = jnp.exp(s - jnp.max(s, axis=1, keepdims=True))
+        prob = (e / jnp.sum(e, axis=1, keepdims=True)).astype(bf16)
+        mixed = dot(prob, value).astype(bf16)
+        for g in range(2):
+            ring[me, g, :, lanes] = mixed[g * half:(g + 1) * half]
+
+    depth = n_pop // 2
+
+    def hop(direction, step, g):
+        at = pop_at(my_r - step if direction == 0 else my_r + step)
+        return pltpu.make_async_remote_copy(
+            src_ref=ring.at[at, g], dst_ref=ring.at[at, g],
+            send_sem=ring_send.at[direction, step, g], recv_sem=ring_recv.at[direction, step, g],
+            device_id={"pop": right if direction == 0 else left}, device_id_type=MESH,
+        )
+
+    def hops(direction, step, g):
+        return step < depth - 1 or (step == depth - 1 and g == direction)
+
+    def term_copy(at, slot, block, i):
+        return pltpu.make_async_remote_copy(
+            src_ref=terms.at[at, block], dst_ref=terms_in.at[mc, at],
+            send_sem=term_send.at[at, block], recv_sem=term_recv.at[mc, at],
+            device_id={"mp": block}, device_id_type=MESH,
+        )
+
+    per_half = n_mp // 2
+
+    def project(at, g):
+        x = ring[at, g]
+        low = dot(x, pack, ((1,), (1,)))
+        r = lax.broadcasted_iota(jnp.int32, low.shape, 0) // own_tok + g * (n_pop // 2)
+        c = lax.broadcasted_iota(jnp.int32, low.shape, 1)
+        keep = (c // PACK == r) & (lax.rem(c, PACK) >= RANK) & (lax.rem(c, PACK) < 2 * RANK)
+        low = jnp.where(keep, low, 0.0)
+        y = dot(x, wo_ref[...])
+        for piece in split3(low):
+            y = y + dot(piece, shifted[...])
+        y = y.astype(bf16)
+        for j in range(per_half):
+            block = g * per_half + j
+            terms[at, block] = y[j * per_mp:(j + 1) * per_mp]
+
+            @pl.when(mc != block)
+            def _():
+                term_copy(at, None, block, None).start()
+
+            @pl.when(mc == block)
+            def _():
+                terms_in[block, at] = terms[at, block]
+
+    for g in range(2):
+        for direction in range(2):
+            hop(direction, 0, g).start()
+    for g in range(2):
+        project(me, g)
+    for step in range(depth):
+        for g in range(2):
+            for direction in range(2):
+                if hops(direction, step, g):
+                    hop(direction, step, g).wait_recv()
+                    if hops(direction, step + 1, g):
+                        hop(direction, step + 1, g).start()
+        for g in range(2):
+            for direction in range(2):
+                if hops(direction, step, g):
+                    project(pop_at(my_r - 1 - step if direction == 0 else my_r + 1 + step), g)
+
+    @pl.when(mc != owner)
+    def _():
+        target_copy(1).wait_recv()
+
+    for i in range(1, n_mp):
+        source = lax.rem(mc + i, n_mp)
+        for at in range(n_pop):
+            pltpu.make_async_remote_copy(
+                src_ref=terms.at[at, 0], dst_ref=terms_in.at[source, at],
+                send_sem=term_send.at[at, 0], recv_sem=term_recv.at[source, at],
+                device_id={"mp": source}, device_id_type=MESH,
+            ).wait_recv()
+
+    members = n_pop // n_mp
+    lane_row = lax.broadcasted_iota(jnp.int32, (1, 128), 1)
+    mine = jnp.zeros((1, 128), f32)
+    for k in range(members):
+        acc = jnp.zeros((own_tok, cols), f32)
+        for at in range(n_pop):
+            span = slice(k * own_tok, (k + 1) * own_tok)
+            out = terms_in[0, at, span].astype(f32)
+            for c in range(1, n_mp):
+                out = out + terms_in[c, at, span].astype(f32)
+            diff = out - target[at * own_tok:(at + 1) * own_tok].astype(f32)
+            acc = acc + diff * diff
+        value_k = jnp.sum(jnp.sum(acc, axis=1, keepdims=True), axis=0, keepdims=True)
+        mine = mine + jnp.where(lane_row == mc * members + k, value_k, 0.0)
+
+    my_id = mc * n_pop + me
+    errs[my_id] = mine
+
+    def err_copy(i):
+        other = lax.rem(my_id + i, n_dev)
+        return pltpu.make_async_remote_copy(
+            src_ref=errs.at[my_id], dst_ref=errs.at[my_id],
+            send_sem=err_send.at[i], recv_sem=err_recv.at[i],
+            device_id={"pop": lax.rem(other, n_pop), "mp": other // n_pop}, device_id_type=MESH,
+        )
+
+    def err_start(i, carry):
+        err_copy(i).start()
+        return carry
+
+    def err_wait(i, carry):
+        err_copy(i).wait_recv()
+        return carry
+
+    lax.fori_loop(1, n_dev, err_start, 0)
+    pack_out[...] = pack
+    for i in range(1, n_pop):
+        for copy in to_pop(i):
+            copy.wait_send()
+    for step in range(depth):
+        for g in range(2):
+            for direction in range(2):
+                if hops(direction, step, g):
+                    hop(direction, step, g).wait_send()
+    for block in range(n_mp):
+        @pl.when(mc != block)
+        def _():
+            for at in range(n_pop):
+                term_copy(at, None, block, None).wait_send()
+
+    @pl.when(mc == owner)
+    def _():
+        for i in range(1, n_mp):
+            target_copy(i).wait_send()
+
+    lax.fori_loop(1, n_dev, err_wait, 0)
+    error = errs[0]
+    for i in range(1, n_dev):
+        error = error + errs[i]
+    live = lane_row < n_pop
+    fitness = -(error / (tok * width))
+    mean = jnp.sum(jnp.where(live, fitness, 0.0), axis=1, keepdims=True) / n_pop
+    dev = jnp.where(live, fitness - mean, 0.0)
+    spread = jnp.sum(dev * dev, axis=1, keepdims=True) / n_pop
+    weight = dev / jnp.sqrt(spread + spread_floor)
+    stat_out[...] = jnp.concatenate(
+        [fitness, weight, jnp.zeros((6, 128), f32)], axis=0
+    )
+
+    def err_drain(i, carry):
+        err_copy(i).wait_send()
+        return carry
+
+    lax.fori_loop(1, n_dev, err_drain, 0)
+
+
+def grad_kernel(pack_ref, stat_ref, gq_ref, go_ref):
+    pack = pack_ref[...]
+    rows = pack.shape[0]
+    cols = go_ref.shape[1]
+    shifted = shift_half(pack)
+    row = lax.broadcasted_iota(jnp.int32, (rows, 128), 0)
+    lane = lax.broadcasted_iota(jnp.int32, (rows, 128), 1)
+    per_row = jnp.sum(jnp.where(lane == row // PACK, stat_ref[1:2, :], 0.0), axis=1, keepdims=True)
+    per_row = per_row / (noise_scale * noise_scale)
+    kind = lax.rem(lax.broadcasted_iota(jnp.int32, (rows, 1), 0), PACK)
+    wq = jnp.where(kind < RANK, per_row, 0.0)
+    wo = jnp.where((kind >= RANK) & (kind < 2 * RANK), per_row, 0.0)
+    small = shifted[:, :cols]
+    for which, weight in ((0, wq), (1, wo)):
+        scaled = split3(small.astype(f32) * weight)
+        if which == 0:
+            gq_ref[...] = sum(dot(s, pack, ((0,), (0,))) for s in scaled)
+        else:
+            go_ref[...] = sum(dot(pack, s, ((0,), (0,))) for s in scaled)
+
+
+def per_device_fast(
+    n_pop, n_mp,
+    tokens, target, w_query, w_key, w_value, w_out,
+    query_left_factors, query_right_factors, o_left, o_right, member_ids,
+):
+    tok, width = tokens.shape
+    rows_q, feats = w_query.shape
+    cols = w_out.shape[1]
+    own_tok = tok // n_pop
+    rows = n_pop * own_tok
+    me = lax.axis_index("pop")
+    factor = (noise_scale * (1 - 2 * (member_ids % 2))).astype(bf16)[0]
+    tok_cols = lax.dynamic_slice(tokens, (0, me * rows_q), (tok, rows_q))
+    ratio = feats // cols
+    tgt = lax.dynamic_slice(target, (0, lax.rem(me, ratio) * cols), (tok, cols))
+    qr = query_right_factors[0] * factor
+    olt = o_left[0].T
+    qlt = query_left_factors[0].T
+    orr = o_right[0] * factor
+    every = lambda x: jnp.broadcast_to(x[None], (n_pop,) + x.shape)
+    blocks = lambda x: jnp.pad(
+        x.reshape(RANK, n_pop, cols).transpose(1, 0, 2), ((0, 0), (0, 0), (0, feats - cols))
+    )
+    pkg = jnp.concatenate([every(qr), every(olt), blocks(qlt), blocks(orr)], axis=1)
+    qlt16 = jnp.pad(qlt, ((0, PACK - RANK), (0, 0)))
+    cosine, sine = rope_tables(tok, HEAD_DIM)
+    vmem = pl.BlockSpec(memory_space=pltpu.VMEM)
+    dma = pltpu.SemaphoreType.DMA
+    depth = n_pop // 2
+    n_dev = n_pop * n_mp
+    pack, stat = pl.pallas_call(
+        functools.partial(forward_kernel, n_pop, n_mp, width),
+        name="forward",
+        out_shape=(
+            jax.ShapeDtypeStruct((n_pop * PACK, feats), bf16),
+            jax.ShapeDtypeStruct((8, 128), f32),
+        ),
+        in_specs=[vmem] * 11,
+        out_specs=(vmem, vmem),
+        scratch_shapes=[
+            pltpu.VMEM((n_pop, own_tok, feats), LINK),
+            pltpu.VMEM((n_pop, own_tok, feats), LINK),
+            pltpu.VMEM((n_pop, own_tok, 128), bf16),
+            pltpu.VMEM((n_pop, own_tok, 128), bf16),
+            pltpu.VMEM((n_pop, PACK, feats), bf16),
+            pltpu.VMEM((n_pop, 2, rows // 2, feats), bf16),
+            pltpu.VMEM((n_pop, n_mp, rows // n_mp, cols), bf16),
+            pltpu.VMEM((n_mp, n_pop, rows // n_mp, cols), bf16),
+            pltpu.VMEM((tok, cols), bf16),
+            pltpu.VMEM((n_dev, 1, 128), f32),
+            pltpu.VMEM((n_pop * PACK, cols), bf16),
+            dma((n_pop,)), dma((n_pop,)), dma((n_pop,)), dma((n_pop,)), dma((n_pop,)), dma((n_pop,)),
+            dma((2, depth, 2)), dma((2, depth, 2)),
+            dma((n_pop, n_mp)), dma((n_mp, n_pop)),
+            dma((n_mp,)), dma,
+            dma((n_dev,)), dma((n_dev,)),
+        ],
+        compiler_params=pltpu.CompilerParams(
+            collective_id=0, has_side_effects=True, vmem_limit_bytes=48 * 1024 * 1024
+        ),
+    )(tokens, tok_cols, w_query, w_key, w_value, w_out, qlt16, pkg, tgt,
+      jnp.asarray(cosine), jnp.asarray(sine))
+    grad_query, grad_out = pl.pallas_call(
+        grad_kernel,
+        name="grads",
+        out_shape=(
+            jax.ShapeDtypeStruct((cols, feats), f32),
+            jax.ShapeDtypeStruct((feats, cols), f32),
+        ),
+        in_specs=[vmem, vmem],
+        out_specs=(vmem, vmem),
+    )(pack, stat)
+    fitness = lax.dynamic_slice(stat[0], (me,), (1,))
+    return grad_query, grad_out, fitness
 
 
 def tables(count, head_size):
@@ -50,7 +456,7 @@
     tok = tokens.shape[0]
     local_feats = w_query.shape[1]
     local_kv = w_key.shape[1] // HEAD_DIM
-    group = HEADS // KV_HEADS
+    group = group_of(w_query, w_key)
     local_heads = local_kv * group
     slots = query_left_factors.shape[0]
     scale = HEAD_DIM ** (-0.5)
@@ -107,7 +513,7 @@
     ).astype(jnp.float32)
     diff = output - target.astype(jnp.float32)[None]
     errors = lax.psum(jnp.sum(diff * diff, axis=(1, 2)), "mp")
-    fitness = -(errors / (tok * D))
+    fitness = -(errors / (tok * tokens.shape[1]))
     count = slots * lax.axis_size("pop")
     mean = lax.psum(jnp.sum(fitness), "pop") / count
     spread = lax.psum(jnp.sum((fitness - mean) * (fitness - mean)), "pop") / count
@@ -133,6 +539,23 @@
     right_o = cols_o.astype(jnp.float32).reshape(whole_population * RANK, cols_o.shape[2])
     grad_out = jnp.dot(output_left_factor, right_o, precision=lax.Precision.HIGHEST) / noise_scale
     return (grad_query, grad_out, fitness)
+
+
+def group_of(w_query, w_key):
+    return w_query.shape[1] // w_key.shape[1]
+
+
+def pick(args, n_pop, n_mp):
+    tok = args[0].shape[0]
+    kernel = (
+        args[6].shape[0] == n_pop
+        and n_pop % (2 * n_mp) == 0
+        and n_mp % 2 == 0
+        and n_pop * PACK <= 128
+        and tok % (n_pop * PACK) == 0
+        and args[3].shape[1] == n_mp * HEAD_DIM
+    )
+    return functools.partial(per_device_fast, n_pop, n_mp) if kernel else per_device
 
 
 def solution(mesh):
@@ -149,10 +572,15 @@
         P("pop", None, None),
         P("pop"),
     )
-    return jax.shard_map(
-        per_device,
-        mesh=mesh,
-        in_specs=placed,
-        out_specs=(P("pop", "mp"), P("mp", "pop"), P("pop")),
-        check_vma=False,
-    )
+    n_pop, n_mp = mesh.shape["pop"], mesh.shape["mp"]
+
+    def whole(*args):
+        return jax.shard_map(
+            pick(args, n_pop, n_mp),
+            mesh=mesh,
+            in_specs=placed,
+            out_specs=(P("pop", "mp"), P("mp", "pop"), P("pop")),
+            check_vma=False,
+        )(*args)
+
+    return whole

time: 466 us -> 111 us (0.24)
  waiting for transfers between devices: 184 us -> 0 us
  blocking collectives: 127 us -> 0 us
  Pallas kernels: 0 us -> 93.4 us
  other arithmetic: 53.7 us -> 1.6 us
  local copies, waits for them, and re-layouts: 46.4 us -> 13.8 us
  matrix products: 24.7 us -> 0 us
  between operations: 19.6 us -> 1.42 us
  starting transfers between devices: 9.34 us -> 0 us
    all_gather x2 -> x0, waiting for transfers between devices: 182 us -> none  [the longest x1 101 us: per_device(): lax.all_gather(w_query, 'pop', axis=0, tiled=True)]
    pallas_call x0 -> x2, Pallas kernels: none -> 93.4 us  [the longest x1 89.5 us: per_device_fast(): pl.pallas_call(functools.partial(forward_kernel, n_pop, n_mp, width), nam...]
    all_gather x2 -> x0, blocking collectives: 62 us -> none  [the longest x1 31.3 us: per_device(): lax.all_gather(o_left, 'pop', axis=0, tiled=True)]
    psum x3 -> x0, blocking collectives: 46.3 us -> none  [the longest x1 21.8 us: per_device(): mean = lax.psum(jnp.sum(fitness), 'pop') / count]
    unnamed x3 -> x0, other arithmetic: 43.4 us -> none
    unnamed x37 -> x18, local copies, waits for them, and re-layouts: 38 us -> 8.65 us
    dot_general x10 -> x0, matrix products: 24.7 us -> none  [the longest x1 4.93 us: per_device(): jnp.einsum('mtf,fe->mte', mixed, lax.all_gather(w_out, 'pop', axis=1, til...]
    unnamed x1 -> x0, blocking collectives: 19.1 us -> none
  transfers between devices with their start and end apart: 5 -> 0, of which waited for: 2 -> 0; matrix products, arithmetic and copies ran while one was open for 19% -> 0% of each run, Pallas kernels for 0% -> 0%
where the time goes in v1:
time: 111 us; the launch traced here: 110 us
  Pallas kernels  93.4 us (84%)
  local copies, waits for them, and re-layouts  13.8 us (12%)
  other arithmetic  1.6 us (1%)
  between operations  1.42 us (1%)
    pallas_call x1, Pallas kernels, per_device_fast(): pl.pallas_call(functools.partial(forward_kernel, n_pop, n_mp, width), nam...  89.5 us
    unnamed x18, local copies, waits for them, and re-layouts  8.65 us
    pallas_call x1, Pallas kernels, per_device_fast(): pl.pallas_call(grad_kernel, name='grads', out_shape=(jax.ShapeDtypeStruct...  3.9 us

profile of v1, /device:TPU:0, one launch (start us, length us, event | category | flops | bytes accessed | tf_op | source)
XLA Modules:
  0.0 110.3 jit_solution(16689656806797990970)
XLA Ops:
  1.3 0.7 multiply_bitcast_fusion
  2.0 0.8 broadcast_multiply_fusion
  2.8 0.1 mul.36
  2.9 0.0 copy-start
  2.9 0.0 copy-start.1
  2.9 1.0 reshape.17
  4.0 0.7 broadcast_in_dim.16
  4.7 0.1 fusion.4.pkg_ref
  4.8 1.4 %pad.11.qlt_ref = bf16[16,3584]{1,0:T(8,128)(2,1)} pad(bf16[4,3584]{1,0:T(4,128)(2,1)} %bitcast.15, bf16[]{:T(256)} %constant.41.clone.1), padding=0_12x0_0 | pad | bytes 143362 | tf_op jit(solution)/shard_map/jit(_pad)/pad | solution.py:374
  6.2 1.3 %constant_dynamic-slice_fusion.1 = (bf16[256,448]{1,0:T(8,128)(2,1)S(1)}, bf16[256,448]{1,0:T(8,128)(2,1)S(1)}) fusion(bf16[256,896]{1,0:T(8,128)(2,1)} %param.14, s32[]{:T(128)S(6)} %select_n.18, bf16[256,3584]{1,0:T(8,128)(2,1)} %tok_ref.1, s32[]{:T(128)S(6)} %select_n.16), kind=kLoop, calls=%fused_computation.13 | loop fusion | bytes 917512 | tf_op jit(solution)/shard_map/dynamic_slice | solution.py:364
  7.6 1.5 %copy.20.wo_ref = bf16[896,448]{1,0:T(8,128)(2,1)S(1)} copy(bf16[896,448]{0,1:T(8,128)(2,1)} %param.18) | data formatting | bytes 1605632 | tf_op args[5]
  9.1 0.0 copy-done
  9.1 0.0 copy-done.1
  9.1 0.0 copy-start.2
  9.1 1.1 %copy-done.2 = bf16[448,896]{1,0:T(8,128)(2,1)S(1)} copy-done((bf16[448,896]{1,0:T(8,128)(2,1)S(1)}, bf16[448,896]{1,0:T(8,128)(2,1)}, u32[]{:S(2)}) %copy-start.2) | copy-done | bytes 802840
  10.2 0.0 copy-start.3
  10.2 0.9 copy-done.3
  11.1 0.0 copy-start.5
  11.1 0.9 copy-done.5
  12.0 0.0 copy-start.6
  12.0 0.9 copy-done.6
  12.9 89.5 %forward.1 = (bf16[128,896]{1,0:T(8,128)(2,1)S(1)}, f32[8,128]{1,0:T(8,128)S(1)}) custom-call(bf16[256,3584]{1,0:T(8,128)(2,1)} %tok_ref.1, bf16[256,448]{1,0:T(8,128)(2,1)S(1)} %get-tuple-element.20.tokp_ref, bf16[448,896]{1,0:T(8,128)(2,1)S(1)} %copy-done.2, bf16[3584,128]{1,0:T(8,128)(2,1)S(1)} %copy-done, bf16[3584,128]{1,0:T(8,128)(2,1)S(1)} %copy-done.1, ...), custom_call_target="tpu_custom_call" | custom-call | tf_op jit(solution)/shard_map/forward/pallas_call | solution.py:380
  102.5 0.0 copy-start.4
  102.5 0.7 copy-done.4
  103.2 0.0 copy-start.7
  103.2 0.6 constant_dynamic-slice_fusion
  103.8 0.0 copy-done.7
  103.8 3.9 %grads.1 = (f32[448,896]{1,0:T(8,128)}, f32[896,448]{1,0:T(8,128)}) custom-call(bf16[128,896]{1,0:T(8,128)(2,1)} %copy-done.4, f32[8,128]{1,0:T(8,128)} %copy-done.7), custom_call_target="tpu_custom_call" | custom-call | tf_op jit(solution)/shard_map/grads/pallas_call | solution.py:412
  107.7 2.6 %copy.21 = f32[896,448]{0,1:T(8,128)} copy(f32[896,448]{1,0:T(8,128)} %get-tuple-element.15) | data formatting | bytes 3211264
  (3 shorter events, 0.1 us)
Async XLA Ops:
  2.9 6.2 %copy-start = (bf16[3584,128]{1,0:T(8,128)(2,1)S(1)}, bf16[3584,128]{1,0:T(8,128)(2,1)}, u32[]{:S(2)}) copy-start(bf16[3584,128]{1,0:T(8,128)(2,1)} %wk_ref.1) | copy-start | bytes 2752516
  2.9 6.2 %copy-start.1 = (bf16[3584,128]{1,0:T(8,128)(2,1)S(1)}, bf16[3584,128]{1,0:T(8,128)(2,1)}, u32[]{:S(2)}) copy-start(bf16[3584,128]{1,0:T(8,128)(2,1)} %wv_ref.1) | copy-start | bytes 2752516
  9.1 1.1 %copy-start.2 = (bf16[448,896]{1,0:T(8,128)(2,1)S(1)}, bf16[448,896]{1,0:T(8,128)(2,1)}, u32[]{:S(2)}) copy-start(bf16[448,896]{1,0:T(8,128)(2,1)} %wq_ref.1) | copy-start | bytes 2408452
  10.2 0.9 copy-start.3
  11.1 0.9 copy-start.5
  12.0 0.9 copy-start.6
  102.5 0.7 copy-start.4
  103.2 0.6 copy-start.7

commit v2 on v1

--- a/solution.py
+++ b/solution.py
@@ -11,8 +11,8 @@
 
 HEAD_DIM = 128
 RANK = 4
-PACK = 16
-LINK = jnp.float32
+PACK = 8
+LINK = jnp.bfloat16
 
 noise_scale = 0.5
 rope_base = 1000000.0
@@ -45,20 +45,15 @@
     return hi, mid, low
 
 
-def shift_half(pack):
-    rows = pack.shape[0]
-    row = lax.broadcasted_iota(jnp.int32, (rows, rows), 0)
-    col = lax.broadcasted_iota(jnp.int32, (rows, rows), 1)
-    perm = ((col == row + PACK // 2) & (row % PACK < PACK // 2)).astype(bf16)
-    return dot(perm, pack).astype(bf16)
-
-
 def forward_kernel(
     n_pop, n_mp, width,
-    tok_ref, tokp_ref, wq_ref, wk_ref, wv_ref, wo_ref, qlt_ref, pkg_ref, tgt_ref, cos_ref, sin_ref,
-    pack_out, stat_out,
-    part, parts_in, lowq, lowq_in, packs, ring, terms, terms_in, target, errs, shifted,
-    base_send, base_recv, lowq_send, lowq_recv, pack_send, pack_recv,
+    tok_hbm, wq_hbm, wk_hbm, wv_hbm, wo_hbm, tgt_hbm, ql_ref, qr_ref, ol_ref, or_ref, id_ref,
+    cos_ref, sin_ref,
+    pack_a_out, pack_b_out, stat_out,
+    tok_ref, wq_ref, wk_ref, wv_ref, wo_ref, tgt_ref,
+    part, parts_in, lowq, lowq_in, mine_a, packs_a, mine_b, packs_b, ring_a, ring_b,
+    terms, terms_in, tgt_own, target, errs, load_sem,
+    base_send, base_recv, lowq_send, lowq_recv, a_send, a_recv, b_send, b_recv,
     ring_send, ring_recv, term_send, term_recv, tgt_send, tgt_recv, err_send, err_recv,
 ):
     me = lax.axis_index("pop")
@@ -67,10 +62,21 @@
     tok, feats = part.shape[0] * part.shape[1], part.shape[2]
     own_tok = tok // n_pop
     rows = n_pop * own_tok
-    half = rows // 2
     per_mp = rows // n_mp
     heads = feats // HEAD_DIM
-    cols = wo_ref.shape[1]
+    cols = wo_ref.shape[0]
+    members = n_pop // n_mp
+    odd = lax.rem(me, 2) == 1
+
+    loads = [
+        pltpu.make_async_copy(src, dst, load_sem.at[i])
+        for i, (src, dst) in enumerate((
+            (tok_hbm, tok_ref), (wq_hbm, wq_ref), (wk_hbm, wk_ref), (wv_hbm, wv_ref),
+            (tgt_hbm, tgt_ref), (wo_hbm, wo_ref),
+        ))
+    ]
+    for load in loads:
+        load.start()
 
     barrier = pltpu.get_barrier_semaphore()
 
@@ -85,146 +91,197 @@
 
     lax.fori_loop(1, n_dev, greet, 0)
 
-    part[...] = dot(tokp_ref[...], wq_ref[...]).reshape(part.shape).astype(part.dtype)
-    low = dot(tok_ref[...], qlt_ref[...], ((1,), (1,))).astype(bf16)
+    sign = 1 - 2 * lax.rem(id_ref[0], 2)
+    factor = noise_scale * sign.astype(f32)
+    mine_a[...] = jnp.concatenate(
+        [qr_ref[...].astype(f32) * factor, ol_ref[...].astype(f32)], axis=0
+    ).astype(bf16)
+    both = jnp.concatenate(
+        [ql_ref[...].astype(f32), or_ref[...].astype(f32) * factor], axis=0
+    )
+    for q in range(n_pop):
+        mine_b[q] = both[:, q * cols:(q + 1) * cols].astype(bf16)
+
+    loads[0].wait()
+    loads[1].wait()
+    window = tok_ref[:, pl.ds(pl.multiple_of(me // 2 * 2 * cols, 128), 2 * cols)]
+    wq = wq_ref[...]
+    first, second = window[:, :cols], window[:, cols:]
+    part[...] = dot(jnp.where(odd, second, first), wq).reshape(part.shape).astype(part.dtype)
+    low = dot(tok_ref[...], both.astype(bf16), ((1,), (1,))).astype(bf16)
     row = lax.broadcasted_iota(jnp.int32, (PACK, 128), 0)
     lane = lax.broadcasted_iota(jnp.int32, (PACK, 128), 1)
-    spread_lanes = (lane == me * PACK + row).astype(bf16)
+    spread_lanes = ((lane == me * PACK + row) & (row < RANK)).astype(bf16)
     lowq[...] = dot(low, spread_lanes).astype(bf16).reshape(lowq.shape)
     parts_in[me] = part[me]
     lowq_in[me] = lowq[me]
-    packs[me] = pkg_ref[me]
+    packs_a[me] = mine_a[...]
+    packs_b[me] = mine_b[me]
 
     pl.semaphore_wait(barrier, n_dev - 1)
 
-    def to_pop(i):
+    def to_pop(i, kind):
         other = lax.rem(me + i, n_pop)
-        source = lax.rem(me + n_pop - i, n_pop)
-        out = []
-        for src, dst, send, recv in (
-            (part, parts_in, base_send, base_recv),
-            (lowq, lowq_in, lowq_send, lowq_recv),
-            (pkg_ref, packs, pack_send, pack_recv),
-        ):
-            out.append(
-                (
-                    pltpu.make_async_remote_copy(
-                        src_ref=src.at[other], dst_ref=dst.at[me], send_sem=send.at[i],
-                        recv_sem=recv.at[i], device_id={"pop": other}, device_id_type=MESH,
-                    )
-                )
-            )
-        return out
-
-    for i in range(1, n_pop):
-        for copy in to_pop(i):
-            copy.start()
+        src, dst, send, recv = (
+            (part.at[other], parts_in, base_send, base_recv),
+            (lowq.at[other], lowq_in, lowq_send, lowq_recv),
+            (mine_a, packs_a, a_send, a_recv),
+            (mine_b.at[other], packs_b, b_send, b_recv),
+        )[kind]
+        return pltpu.make_async_remote_copy(
+            src_ref=src, dst_ref=dst.at[me], send_sem=send.at[i],
+            recv_sem=recv.at[i], device_id={"pop": other}, device_id_type=MESH,
+        )
+
+    for kind in (0, 1, 2, 3):
+        for i in range(1, n_pop):
+            to_pop(i, kind).start()
 
     owner = me // (n_pop // n_mp)
 
     def target_copy(i):
         return pltpu.make_async_remote_copy(
-            src_ref=tgt_ref, dst_ref=target, send_sem=tgt_send.at[i], recv_sem=tgt_recv,
+            src_ref=tgt_own, dst_ref=target, send_sem=tgt_send.at[i], recv_sem=tgt_recv,
             device_id={"mp": lax.rem(mc + i, n_mp)}, device_id_type=MESH,
         )
 
+    loads[4].wait()
+
     @pl.when(mc == owner)
     def _():
+        tgt_own[...] = jnp.where(odd, tgt_ref[:, cols:], tgt_ref[:, :cols])
         for i in range(1, n_mp):
             target_copy(i).start()
-        target[...] = tgt_ref[...]
-
+        target[...] = tgt_own[...]
+
+    loads[2].wait()
+    loads[3].wait()
     cosine, sine = cos_ref[...], sin_ref[...]
     key = dot(tok_ref[...], wk_ref[...])
     key = (key * cosine + pltpu.roll(key, HEAD_DIM // 2, 1) * sine).astype(bf16)
     value = dot(tok_ref[...], wv_ref[...]).astype(bf16)
 
-    for i in range(1, n_pop):
-        for copy in to_pop(i):
-            copy.wait_recv()
-
-    pack = packs[...].reshape(n_pop * PACK, feats)
-    shifted[...] = shift_half(pack[:, :cols]) if cols % 128 == 0 else shift_half(pack)[:, :cols]
-
-    def pop_at(r):
-        r = lax.rem(r + 2 * n_pop, n_pop)
-        return jnp.where(r < n_pop // 2, 2 * r, 2 * (n_pop - 1 - r) + 1)
-
-    my_r = jnp.where(lax.rem(me, 2) == 0, me // 2, n_pop - 1 - me // 2)
-    right, left = pop_at(my_r + 1), pop_at(my_r - 1)
-
-    total = parts_in[0].astype(f32)
-    for i in range(1, n_pop):
-        total = total + parts_in[i].astype(f32)
-    low_rows = lowq_in[...].reshape(rows, 128)
     start = pl.multiple_of(me * own_tok, own_tok)
     cos_own = jnp.tile(cos_ref[pl.ds(start, own_tok), :], (n_pop, 1))
     sin_own = jnp.tile(sin_ref[pl.ds(start, own_tok), :], (n_pop, 1))
     token_of = start + lax.rem(lax.broadcasted_iota(jnp.int32, (rows, tok), 0), own_tok)
     causal = token_of >= lax.broadcasted_iota(jnp.int32, (rows, tok), 1)
     scale = HEAD_DIM ** (-0.5)
+
+    for kind in (0, 1, 2):
+        for i in range(1, n_pop):
+            to_pop(i, kind).wait_recv()
+
+    def pop_at(r):
+        r = lax.rem(r + 2 * n_pop, n_pop)
+        return jnp.where(r < n_pop // 2, 2 * r, 2 * (n_pop - 1 - r) + 1)
+
+    my_r = jnp.where(odd, n_pop - 1 - me // 2, me // 2)
+    right, left = pop_at(my_r + 1), pop_at(my_r - 1)
+
+    depth = n_pop // 2
+    rings = (ring_a, ring_b)
+
+    def hop(direction, step, g):
+        at = pop_at(my_r - step if direction == 0 else my_r + step)
+        return pltpu.make_async_remote_copy(
+            src_ref=rings[g].at[at], dst_ref=rings[g].at[at],
+            send_sem=ring_send.at[direction, step, g], recv_sem=ring_recv.at[direction, step, g],
+            device_id={"pop": right if direction == 0 else left}, device_id_type=MESH,
+        )
+
+    def hops(direction, step, g):
+        return step < depth - 1 or (step == depth - 1 and g == direction)
+
+    pack_a = jnp.concatenate([packs_a[i].astype(f32) for i in range(n_pop)], axis=0).astype(bf16)
+    low_rows = lowq_in[...].reshape(rows, 128)[:, :n_pop * PACK]
+    group = ring_a.shape[2] // HEAD_DIM
     for h in range(heads):
         lanes = slice(h * HEAD_DIM, (h + 1) * HEAD_DIM)
-        q = jnp.tile(total[:, lanes], (n_pop, 1)) + dot(low_rows, pack[:, lanes])
+        total = parts_in[0, :, lanes].astype(f32)
+        for i in range(1, n_pop):
+            total = total + parts_in[i, :, lanes].astype(f32)
+        q = jnp.tile(total, (n_pop, 1)) + dot(low_rows, pack_a[:, lanes])
         q = (q * cos_own + pltpu.roll(q, HEAD_DIM // 2, 1) * sin_own).astype(bf16)
         s = dot(q, key, ((1,), (1,))) * scale
         s = jnp.where(causal, s, -1e30)
         e = jnp.exp(s - jnp.max(s, axis=1, keepdims=True))
         prob = (e / jnp.sum(e, axis=1, keepdims=True)).astype(bf16)
         mixed = dot(prob, value).astype(bf16)
-        for g in range(2):
-            ring[me, g, :, lanes] = mixed[g * half:(g + 1) * half]
-
-    depth = n_pop // 2
-
-    def hop(direction, step, g):
-        at = pop_at(my_r - step if direction == 0 else my_r + step)
-        return pltpu.make_async_remote_copy(
-            src_ref=ring.at[at, g], dst_ref=ring.at[at, g],
-            send_sem=ring_send.at[direction, step, g], recv_sem=ring_recv.at[direction, step, g],
-            device_id={"pop": right if direction == 0 else left}, device_id_type=MESH,
-        )
-
-    def hops(direction, step, g):
-        return step < depth - 1 or (step == depth - 1 and g == direction)
-
-    def term_copy(at, slot, block, i):
+        g = 0 if h < group else 1
+        at = h - g * group
+        rings[g][me, :, at * HEAD_DIM:(at + 1) * HEAD_DIM] = mixed
+        if h in (group - 1, heads - 1):
+            for direction in range(2):
+                hop(direction, 0, g).start()
+
+    for i in range(1, n_pop):
+        to_pop(i, 3).wait_recv()
+    pack_b = jnp.concatenate([packs_b[i].astype(f32) for i in range(n_pop)], axis=0).astype(bf16)
+    pack_a_out[...] = pack_a
+    pack_b_out[...] = pack_b
+    loads[5].wait()
+
+    def term_copy(at, block):
         return pltpu.make_async_remote_copy(
             src_ref=terms.at[at, block], dst_ref=terms_in.at[mc, at],
             send_sem=term_send.at[at, block], recv_sem=term_recv.at[mc, at],
             device_id={"mp": block}, device_id_type=MESH,
         )
 
-    per_half = n_mp // 2
-
-    def project(at, g):
-        x = ring[at, g]
-        low = dot(x, pack, ((1,), (1,)))
-        r = lax.broadcasted_iota(jnp.int32, low.shape, 0) // own_tok + g * (n_pop // 2)
-        c = lax.broadcasted_iota(jnp.int32, low.shape, 1)
-        keep = (c // PACK == r) & (lax.rem(c, PACK) >= RANK) & (lax.rem(c, PACK) < 2 * RANK)
+    low_shape = (rows, n_pop * PACK)
+    member_of = lax.broadcasted_iota(jnp.int32, low_shape, 0) // own_tok
+    place = lax.broadcasted_iota(jnp.int32, low_shape, 1)
+    keep = (place // PACK == member_of) & (lax.rem(place, PACK) >= RANK)
+    cut = group * HEAD_DIM
+
+    def project(at):
+        xa, xb = ring_a[at], ring_b[at]
+        nt = ((1,), (1,))
+        low = dot(xa, pack_a[:, :cut], nt) + dot(xb, pack_a[:, cut:], nt)
         low = jnp.where(keep, low, 0.0)
-        y = dot(x, wo_ref[...])
+        y = dot(xa, wo_ref[:, :cut], nt) + dot(xb, wo_ref[:, cut:], nt)
         for piece in split3(low):
-            y = y + dot(piece, shifted[...])
+            y = y + dot(piece, pack_b)
         y = y.astype(bf16)
-        for j in range(per_half):
-            block = g * per_half + j
-            terms[at, block] = y[j * per_mp:(j + 1) * per_mp]
+        for block in range(n_mp):
+            terms[at, block] = y[block * per_mp:(block + 1) * per_mp]
 
             @pl.when(mc != block)
             def _():
-                term_copy(at, None, block, None).start()
+                term_copy(at, block).start()
 
             @pl.when(mc == block)
             def _():
                 terms_in[block, at] = terms[at, block]
 
-    for g in range(2):
-        for direction in range(2):
-            hop(direction, 0, g).start()
-    for g in range(2):
-        project(me, g)
+    def squares(at, totals):
+        for i in range(1, n_mp):
+            source = lax.rem(mc + i, n_mp)
+            pltpu.make_async_remote_copy(
+                src_ref=terms.at[at, 0], dst_ref=terms_in.at[source, at],
+                send_sem=term_send.at[at, 0], recv_sem=term_recv.at[source, at],
+                device_id={"mp": source}, device_id_type=MESH,
+            ).wait_recv()
+        goal = target[pl.ds(pl.multiple_of(at * own_tok, own_tok), own_tok), :].astype(f32)
+        result = []
+        for k in range(members):
+            span = slice(k * own_tok, (k + 1) * own_tok)
+            out = terms_in[0, at, span].astype(f32)
+            for c in range(1, n_mp):
+                out = out + terms_in[c, at, span].astype(f32)
+            diff = out - goal
+            result.append(totals[k] + jnp.sum(diff * diff, axis=0, keepdims=True))
+        return result
+
+    project(me)
+
+    @pl.when(mc != owner)
+    def _():
+        target_copy(1).wait_recv()
+
+    totals = [jnp.zeros((1, cols), f32)] * members
+    done = [me]
     for step in range(depth):
         for g in range(2):
             for direction in range(2):
@@ -232,37 +289,21 @@
                     hop(direction, step, g).wait_recv()
                     if hops(direction, step + 1, g):
                         hop(direction, step + 1, g).start()
-        for g in range(2):
-            for direction in range(2):
-                if hops(direction, step, g):
-                    project(pop_at(my_r - 1 - step if direction == 0 else my_r + 1 + step), g)
-
-    @pl.when(mc != owner)
-    def _():
-        target_copy(1).wait_recv()
-
-    for i in range(1, n_mp):
-        source = lax.rem(mc + i, n_mp)
-        for at in range(n_pop):
-            pltpu.make_async_remote_copy(
-                src_ref=terms.at[at, 0], dst_ref=terms_in.at[source, at],
-                send_sem=term_send.at[at, 0], recv_sem=term_recv.at[source, at],
-                device_id={"mp": source}, device_id_type=MESH,
-            ).wait_recv()
-
-    members = n_pop // n_mp
+        landed = [pop_at(my_r - 1 - step)]
+        if step < depth - 1:
+            landed.append(pop_at(my_r + 1 + step))
+        for at in landed:
+            project(at)
+        for at in done:
+            totals = squares(at, totals)
+        done = landed
+    for at in done:
+        totals = squares(at, totals)
+
     lane_row = lax.broadcasted_iota(jnp.int32, (1, 128), 1)
     mine = jnp.zeros((1, 128), f32)
     for k in range(members):
-        acc = jnp.zeros((own_tok, cols), f32)
-        for at in range(n_pop):
-            span = slice(k * own_tok, (k + 1) * own_tok)
-            out = terms_in[0, at, span].astype(f32)
-            for c in range(1, n_mp):
-                out = out + terms_in[c, at, span].astype(f32)
-            diff = out - target[at * own_tok:(at + 1) * own_tok].astype(f32)
-            acc = acc + diff * diff
-        value_k = jnp.sum(jnp.sum(acc, axis=1, keepdims=True), axis=0, keepdims=True)
+        value_k = jnp.sum(totals[k], axis=1, keepdims=True)
         mine = mine + jnp.where(lane_row == mc * members + k, value_k, 0.0)
 
     my_id = mc * n_pop + me
@@ -285,10 +326,9 @@
         return carry
 
     lax.fori_loop(1, n_dev, err_start, 0)
-    pack_out[...] = pack
-    for i in range(1, n_pop):
-        for copy in to_pop(i):
-            copy.wait_send()
+    for kind in range(4):
+        for i in range(1, n_pop):
+            to_pop(i, kind).wait_send()
     for step in range(depth):
         for g in range(2):
             for direction in range(2):
@@ -298,7 +338,7 @@
         @pl.when(mc != block)
         def _():
             for at in range(n_pop):
-                term_copy(at, None, block, None).wait_send()
+                term_copy(at, block).wait_send()
 
     @pl.when(mc == owner)
     def _():
@@ -326,25 +366,20 @@
     lax.fori_loop(1, n_dev, err_drain, 0)
 
 
-def grad_kernel(pack_ref, stat_ref, gq_ref, go_ref):
-    pack = pack_ref[...]
-    rows = pack.shape[0]
-    cols = go_ref.shape[1]
-    shifted = shift_half(pack)
+def grad_kernel(a_ref, b_ref, stat_ref, gq_ref, got_ref):
+    pack_a = a_ref[...]
+    pack_b = b_ref[...].astype(f32)
+    rows = pack_a.shape[0]
     row = lax.broadcasted_iota(jnp.int32, (rows, 128), 0)
     lane = lax.broadcasted_iota(jnp.int32, (rows, 128), 1)
     per_row = jnp.sum(jnp.where(lane == row // PACK, stat_ref[1:2, :], 0.0), axis=1, keepdims=True)
     per_row = per_row / (noise_scale * noise_scale)
     kind = lax.rem(lax.broadcasted_iota(jnp.int32, (rows, 1), 0), PACK)
-    wq = jnp.where(kind < RANK, per_row, 0.0)
-    wo = jnp.where((kind >= RANK) & (kind < 2 * RANK), per_row, 0.0)
-    small = shifted[:, :cols]
-    for which, weight in ((0, wq), (1, wo)):
-        scaled = split3(small.astype(f32) * weight)
-        if which == 0:
-            gq_ref[...] = sum(dot(s, pack, ((0,), (0,))) for s in scaled)
-        else:
-            go_ref[...] = sum(dot(pack, s, ((0,), (0,))) for s in scaled)
+    for out, weight in (
+        (gq_ref, jnp.where(kind < RANK, per_row, 0.0)),
+        (got_ref, jnp.where(kind >= RANK, per_row, 0.0)),
+    ):
+        out[...] = sum(dot(s, pack_a, ((0,), (0,))) for s in split3(pack_b * weight))
 
 
 def per_device_fast(
@@ -353,74 +388,74 @@
     query_left_factors, query_right_factors, o_left, o_right, member_ids,
 ):
     tok, width = tokens.shape
-    rows_q, feats = w_query.shape
+    feats = w_query.shape[1]
     cols = w_out.shape[1]
     own_tok = tok // n_pop
     rows = n_pop * own_tok
     me = lax.axis_index("pop")
-    factor = (noise_scale * (1 - 2 * (member_ids % 2))).astype(bf16)[0]
-    tok_cols = lax.dynamic_slice(tokens, (0, me * rows_q), (tok, rows_q))
-    ratio = feats // cols
-    tgt = lax.dynamic_slice(target, (0, lax.rem(me, ratio) * cols), (tok, cols))
-    qr = query_right_factors[0] * factor
-    olt = o_left[0].T
-    qlt = query_left_factors[0].T
-    orr = o_right[0] * factor
-    every = lambda x: jnp.broadcast_to(x[None], (n_pop,) + x.shape)
-    blocks = lambda x: jnp.pad(
-        x.reshape(RANK, n_pop, cols).transpose(1, 0, 2), ((0, 0), (0, 0), (0, feats - cols))
-    )
-    pkg = jnp.concatenate([every(qr), every(olt), blocks(qlt), blocks(orr)], axis=1)
-    qlt16 = jnp.pad(qlt, ((0, PACK - RANK), (0, 0)))
     cosine, sine = rope_tables(tok, HEAD_DIM)
     vmem = pl.BlockSpec(memory_space=pltpu.VMEM)
+    hbm = pl.BlockSpec(memory_space=pltpu.HBM)
+    smem = pl.BlockSpec(memory_space=pltpu.SMEM)
     dma = pltpu.SemaphoreType.DMA
     depth = n_pop // 2
     n_dev = n_pop * n_mp
-    pack, stat = pl.pallas_call(
+    cut = (feats // HEAD_DIM + 1) // 2 * HEAD_DIM
+    like = lambda x: pltpu.VMEM(x.shape, x.dtype)
+    wot = w_out.T
+    pack_a, pack_b, stat = pl.pallas_call(
         functools.partial(forward_kernel, n_pop, n_mp, width),
         name="forward",
         out_shape=(
             jax.ShapeDtypeStruct((n_pop * PACK, feats), bf16),
+            jax.ShapeDtypeStruct((n_pop * PACK, cols), bf16),
             jax.ShapeDtypeStruct((8, 128), f32),
         ),
-        in_specs=[vmem] * 11,
-        out_specs=(vmem, vmem),
+        in_specs=[hbm] * 6 + [vmem] * 4 + [smem] + [vmem] * 2,
+        out_specs=(vmem, vmem, vmem),
         scratch_shapes=[
+            like(tokens), like(w_query), like(w_key), like(w_value), like(wot), like(target),
             pltpu.VMEM((n_pop, own_tok, feats), LINK),
             pltpu.VMEM((n_pop, own_tok, feats), LINK),
             pltpu.VMEM((n_pop, own_tok, 128), bf16),
             pltpu.VMEM((n_pop, own_tok, 128), bf16),
+            pltpu.VMEM((PACK, feats), bf16),
             pltpu.VMEM((n_pop, PACK, feats), bf16),
-            pltpu.VMEM((n_pop, 2, rows // 2, feats), bf16),
+            pltpu.VMEM((n_pop, PACK, cols), bf16),
+            pltpu.VMEM((n_pop, PACK, cols), bf16),
+            pltpu.VMEM((n_pop, rows, cut), bf16),
+            pltpu.VMEM((n_pop, rows, feats - cut), bf16),
             pltpu.VMEM((n_pop, n_mp, rows // n_mp, cols), bf16),
             pltpu.VMEM((n_mp, n_pop, rows // n_mp, cols), bf16),
             pltpu.VMEM((tok, cols), bf16),
+            pltpu.VMEM((tok, cols), bf16),
             pltpu.VMEM((n_dev, 1, 128), f32),
-            pltpu.VMEM((n_pop * PACK, cols), bf16),
-            dma((n_pop,)), dma((n_pop,)), dma((n_pop,)), dma((n_pop,)), dma((n_pop,)), dma((n_pop,)),
+            dma((6,)),
+            dma((n_pop,)), dma((n_pop,)), dma((n_pop,)), dma((n_pop,)),
+            dma((n_pop,)), dma((n_pop,)), dma((n_pop,)), dma((n_pop,)),
             dma((2, depth, 2)), dma((2, depth, 2)),
             dma((n_pop, n_mp)), dma((n_mp, n_pop)),
             dma((n_mp,)), dma,
             dma((n_dev,)), dma((n_dev,)),
         ],
         compiler_params=pltpu.CompilerParams(
-            collective_id=0, has_side_effects=True, vmem_limit_bytes=48 * 1024 * 1024
+            collective_id=0, has_side_effects=True, vmem_limit_bytes=60 * 1024 * 1024
         ),
-    )(tokens, tok_cols, w_query, w_key, w_value, w_out, qlt16, pkg, tgt,
+    )(tokens, w_query, w_key, w_value, wot, target,
+      query_left_factors[0].T, query_right_factors[0], o_left[0].T, o_right[0], member_ids,
       jnp.asarray(cosine), jnp.asarray(sine))
-    grad_query, grad_out = pl.pallas_call(
+    grad_query, grad_out_t = pl.pallas_call(
         grad_kernel,
         name="grads",
         out_shape=(
             jax.ShapeDtypeStruct((cols, feats), f32),
-            jax.ShapeDtypeStruct((feats, cols), f32),
+            jax.ShapeDtypeStruct((cols, feats), f32),
         ),
-        in_specs=[vmem, vmem],
+        in_specs=[vmem, vmem, vmem],
         out_specs=(vmem, vmem),
-    )(pack, stat)
+    )(pack_a, pack_b, stat)
     fitness = lax.dynamic_slice(stat[0], (me,), (1,))
-    return grad_query, grad_out, fitness
+    return grad_query, grad_out_t.T, fitness
 
 
 def tables(count, head_size):
@@ -549,10 +584,12 @@
     tok = args[0].shape[0]
     kernel = (
         args[6].shape[0] == n_pop
-        and n_pop % (2 * n_mp) == 0
-        and n_mp % 2 == 0
+        and n_pop % n_mp == 0
+        and n_pop % 2 == 0
         and n_pop * PACK <= 128
-        and tok % (n_pop * PACK) == 0
+        and tok % (n_pop * 16) == 0
+        and args[2].shape[1] // n_mp == 2 * args[5].shape[1] // n_pop
+        and args[2].shape[0] == args[5].shape[1]
         and args[3].shape[1] == n_mp * HEAD_DIM
     )
     return functools.partial(per_device_fast, n_pop, n_mp) if kernel else per_device

time: 111 us -> 82.6 us (0.74)
  Pallas kernels: 93.4 us -> 79.8 us
  local copies, waits for them, and re-layouts: 13.8 us -> 1.26 us
  other arithmetic: 1.6 us -> 0 us
    pallas_call x1, Pallas kernels: 89.5 us -> 76 us  [per_device_fast(): pl.pallas_call(functools.partial(forward_kernel, n_pop, n_mp, width), nam...]
    unnamed x18 -> x0, local copies, waits for them, and re-layouts: 8.65 us -> none
    pad x1 -> x0, local copies, waits for them, and re-layouts: 1.41 us -> none  [per_device_fast(): qlt16 = jnp.pad(qlt, ((0, PACK - RANK), (0, 0)))]
    dynamic_slice x1 -> x0, local copies, waits for them, and re-layouts: 1.34 us -> none  [per_device_fast(): tgt = lax.dynamic_slice(target, (0, lax.rem(me, ratio) * cols), (tok, cols))]
where the time goes in v2:
time: 82.6 us; the launch traced here: 82.3 us
  Pallas kernels  79.8 us (97%)
  between operations  1.29 us (2%)
  local copies, waits for them, and re-layouts  1.26 us (2%)
    pallas_call x1, Pallas kernels, per_device_fast(): pl.pallas_call(functools.partial(forward_kernel, n_pop, n_mp, width), nam...  76 us
    pallas_call x1, Pallas kernels, per_device_fast(): pl.pallas_call(grad_kernel, name='grads', out_shape=(jax.ShapeDtypeStruct...  3.81 us

profile of v2, /device:TPU:0, one launch (start us, length us, event | category | flops | bytes accessed | tf_op | source)
XLA Modules:
  0.0 82.3 jit_solution(16103425989473697826)
XLA Ops:
  1.3 76.0 %forward.1 = (bf16[64,896]{1,0:T(8,128)(2,1)}, bf16[64,448]{1,0:T(8,128)(2,1)}, f32[8,128]{1,0:T(8,128)}) custom-call(bf16[256,3584]{1,0:T(8,128)(2,1)} %tok_hbm.1, bf16[448,896]{1,0:T(8,128)(2,1)} %wq_hbm.1, bf16[3584,128]{1,0:T(8,128)(2,1)} %wk_hbm.1, bf16[3584,128]{1,0:T(8,128)(2,1)} %wv_hbm.1, bf16[448,896]{1,0:T(8,128)(2,1)} %bitcast.11, ...), custom_call_target="tpu_custom_call" | custom-call | tf_op jit(solution)/shard_map/forward/pallas_call | solution.py:406
  77.3 3.8 %grads.1 = (f32[448,896]{1,0:T(8,128)}, f32[448,896]{1,0:T(8,128)}) custom-call(bf16[64,896]{1,0:T(8,128)(2,1)} %get-tuple-element.8.a_ref, bf16[64,448]{1,0:T(8,128)(2,1)} %get-tuple-element.9.b_ref, f32[8,128]{1,0:T(8,128)} %get-tuple-element.10.stat_ref), custom_call_target="tpu_custom_call" | custom-call | tf_op jit(solution)/shard_map/grads/pallas_call | solution.py:447
  81.1 0.7 slice.3
  81.8 0.6 constant_dynamic-slice_fusion

commit v3 on v2

--- a/solution.py
+++ b/solution.py
@@ -51,15 +51,17 @@
     cos_ref, sin_ref,
     pack_a_out, pack_b_out, stat_out,
     tok_ref, wq_ref, wk_ref, wv_ref, wo_ref, tgt_ref,
-    part, parts_in, lowq, lowq_in, mine_a, packs_a, mine_b, packs_b, ring_a, ring_b,
+    part_a, part_b, parts_a, parts_b, mine_l, packs_l, mine_q, packs_q, mine_o, packs_o,
+    mine_b, packs_b, ring_a, ring_b,
     terms, terms_in, tgt_own, target, errs, load_sem,
-    base_send, base_recv, lowq_send, lowq_recv, a_send, a_recv, b_send, b_recv,
+    pop_send, pop_recv,
     ring_send, ring_recv, term_send, term_recv, tgt_send, tgt_recv, err_send, err_recv,
 ):
     me = lax.axis_index("pop")
     mc = lax.axis_index("mp")
     n_dev = n_pop * n_mp
-    tok, feats = part.shape[0] * part.shape[1], part.shape[2]
+    tok, feats = tok_ref.shape[0], wq_ref.shape[1]
+    cut = ring_a.shape[2]
     own_tok = tok // n_pop
     rows = n_pop * own_tok
     per_mp = rows // n_mp
@@ -93,49 +95,61 @@
 
     sign = 1 - 2 * lax.rem(id_ref[0], 2)
     factor = noise_scale * sign.astype(f32)
-    mine_a[...] = jnp.concatenate(
-        [qr_ref[...].astype(f32) * factor, ol_ref[...].astype(f32)], axis=0
-    ).astype(bf16)
-    both = jnp.concatenate(
-        [ql_ref[...].astype(f32), or_ref[...].astype(f32) * factor], axis=0
-    )
-    for q in range(n_pop):
-        mine_b[q] = both[:, q * cols:(q + 1) * cols].astype(bf16)
-
     loads[0].wait()
     loads[1].wait()
     window = tok_ref[:, pl.ds(pl.multiple_of(me // 2 * 2 * cols, 128), 2 * cols)]
     wq = wq_ref[...]
     first, second = window[:, :cols], window[:, cols:]
-    part[...] = dot(jnp.where(odd, second, first), wq).reshape(part.shape).astype(part.dtype)
-    low = dot(tok_ref[...], both.astype(bf16), ((1,), (1,))).astype(bf16)
-    row = lax.broadcasted_iota(jnp.int32, (PACK, 128), 0)
-    lane = lax.broadcasted_iota(jnp.int32, (PACK, 128), 1)
-    spread_lanes = ((lane == me * PACK + row) & (row < RANK)).astype(bf16)
-    lowq[...] = dot(low, spread_lanes).astype(bf16).reshape(lowq.shape)
-    parts_in[me] = part[me]
-    lowq_in[me] = lowq[me]
-    packs_a[me] = mine_a[...]
-    packs_b[me] = mine_b[me]
+    base = dot(jnp.where(odd, second, first), wq)
+    part_a[...] = base[:, :cut].reshape(part_a.shape).astype(LINK)
+    part_b[...] = base[:, cut:].reshape(part_b.shape).astype(LINK)
+    mine_q[...] = (qr_ref[...].astype(f32) * factor).astype(bf16)
 
     pl.semaphore_wait(barrier, n_dev - 1)
 
     def to_pop(i, kind):
         other = lax.rem(me + i, n_pop)
-        src, dst, send, recv = (
-            (part.at[other], parts_in, base_send, base_recv),
-            (lowq.at[other], lowq_in, lowq_send, lowq_recv),
-            (mine_a, packs_a, a_send, a_recv),
-            (mine_b.at[other], packs_b, b_send, b_recv),
+        src, dst = (
+            (part_a.at[other], parts_a),
+            (mine_q, packs_q),
+            (mine_l.at[other], packs_l),
+            (part_b.at[other], parts_b),
+            (mine_o, packs_o),
+            (mine_b.at[other], packs_b),
         )[kind]
         return pltpu.make_async_remote_copy(
-            src_ref=src, dst_ref=dst.at[me], send_sem=send.at[i],
-            recv_sem=recv.at[i], device_id={"pop": other}, device_id_type=MESH,
+            src_ref=src, dst_ref=dst.at[me], send_sem=pop_send.at[kind, i],
+            recv_sem=pop_recv.at[kind, i], device_id={"pop": other}, device_id_type=MESH,
         )
 
-    for kind in (0, 1, 2, 3):
+    def to_all(kind):
         for i in range(1, n_pop):
             to_pop(i, kind).start()
+
+    def from_all(kind):
+        for i in range(1, n_pop):
+            to_pop(i, kind).wait_recv()
+
+    to_all(0)
+    to_all(1)
+    ql = ql_ref[...]
+    low = dot(ql, tok_ref[...], ((1,), (1,))).astype(bf16).astype(f32)
+    for q in range(n_pop):
+        mine_l[q] = jnp.concatenate(
+            [low[:, q * own_tok:(q + 1) * own_tok], jnp.zeros((RANK, 128 - own_tok), f32)], axis=1
+        ).astype(bf16)
+    to_all(2)
+    to_all(3)
+    mine_o[...] = ol_ref[...]
+    both = jnp.concatenate([ql.astype(f32), or_ref[...].astype(f32) * factor], axis=0)
+    for q in range(n_pop):
+        mine_b[q] = both[:, q * cols:(q + 1) * cols].astype(bf16)
+    to_all(4)
+    to_all(5)
+    for mine, packs in ((part_a, parts_a), (part_b, parts_b), (mine_l, packs_l), (mine_b, packs_b)):
+        packs[me] = mine[me]
+    packs_q[me] = mine_q[...]
+    packs_o[me] = mine_o[...]
 
     owner = me // (n_pop // n_mp)
 
@@ -168,9 +182,8 @@
     causal = token_of >= lax.broadcasted_iota(jnp.int32, (rows, tok), 1)
     scale = HEAD_DIM ** (-0.5)
 
-    for kind in (0, 1, 2):
-        for i in range(1, n_pop):
-            to_pop(i, kind).wait_recv()
+    for kind in range(3):
+        from_all(kind)
 
     def pop_at(r):
         r = lax.rem(r + 2 * n_pop, n_pop)
@@ -193,31 +206,50 @@
     def hops(direction, step, g):
         return step < depth - 1 or (step == depth - 1 and g == direction)
 
-    pack_a = jnp.concatenate([packs_a[i].astype(f32) for i in range(n_pop)], axis=0).astype(bf16)
-    low_rows = lowq_in[...].reshape(rows, 128)[:, :n_pop * PACK]
+    def stacked(parts, *more):
+        return jnp.concatenate(
+            [p[i].astype(f32) for i in range(n_pop) for p in (parts,) + more], axis=0
+        ).astype(bf16)
+
+    pack_q = stacked(packs_q)
+    ranks = n_pop * RANK
+    eye = (
+        lax.broadcasted_iota(jnp.int32, (ranks, ranks), 0)
+        == lax.broadcasted_iota(jnp.int32, (ranks, ranks), 1)
+    ).astype(bf16)
+    low_rows = dot(stacked(packs_l), eye, ((0,), (0,)))[:own_tok]
+    low_rows = jnp.tile(low_rows, (n_pop, 1))
+    of_rank = lax.broadcasted_iota(jnp.int32, low_rows.shape, 1) // RANK
+    of_row = lax.broadcasted_iota(jnp.int32, low_rows.shape, 0) // own_tok
+    low_rows = jnp.where(of_rank == of_row, low_rows, 0.0).astype(bf16)
     group = ring_a.shape[2] // HEAD_DIM
     for h in range(heads):
         lanes = slice(h * HEAD_DIM, (h + 1) * HEAD_DIM)
-        total = parts_in[0, :, lanes].astype(f32)
+        g = 0 if h < group else 1
+        at = h - g * group
+        here = slice(at * HEAD_DIM, (at + 1) * HEAD_DIM)
+        if h == group:
+            from_all(3)
+        parts = (parts_a, parts_b)[g]
+        total = parts[0, :, here].astype(f32)
         for i in range(1, n_pop):
-            total = total + parts_in[i, :, lanes].astype(f32)
-        q = jnp.tile(total, (n_pop, 1)) + dot(low_rows, pack_a[:, lanes])
+            total = total + parts[i, :, here].astype(f32)
+        q = jnp.tile(total, (n_pop, 1)) + dot(low_rows, pack_q[:, lanes])
         q = (q * cos_own + pltpu.roll(q, HEAD_DIM // 2, 1) * sin_own).astype(bf16)
         s = dot(q, key, ((1,), (1,))) * scale
         s = jnp.where(causal, s, -1e30)
         e = jnp.exp(s - jnp.max(s, axis=1, keepdims=True))
         prob = (e / jnp.sum(e, axis=1, keepdims=True)).astype(bf16)
         mixed = dot(prob, value).astype(bf16)
-        g = 0 if h < group else 1
-        at = h - g * group
-        rings[g][me, :, at * HEAD_DIM:(at + 1) * HEAD_DIM] = mixed
+        rings[g][me, :, here] = mixed
         if h in (group - 1, heads - 1):
             for direction in range(2):
                 hop(direction, 0, g).start()
 
-    for i in range(1, n_pop):
-        to_pop(i, 3).wait_recv()
-    pack_b = jnp.concatenate([packs_b[i].astype(f32) for i in range(n_pop)], axis=0).astype(bf16)
+    from_all(4)
+    from_all(5)
+    pack_a = stacked(packs_q, packs_o)
+    pack_b = stacked(packs_b)
     pack_a_out[...] = pack_a
     pack_b_out[...] = pack_b
     loads[5].wait()
@@ -233,7 +265,6 @@
     member_of = lax.broadcasted_iota(jnp.int32, low_shape, 0) // own_tok
     place = lax.broadcasted_iota(jnp.int32, low_shape, 1)
     keep = (place // PACK == member_of) & (lax.rem(place, PACK) >= RANK)
-    cut = group * HEAD_DIM
 
     def project(at):
         xa, xb = ring_a[at], ring_b[at]
@@ -326,7 +357,7 @@
         return carry
 
     lax.fori_loop(1, n_dev, err_start, 0)
-    for kind in range(4):
+    for kind in range(6):
         for i in range(1, n_pop):
             to_pop(i, kind).wait_send()
     for step in range(depth):
@@ -366,20 +397,34 @@
     lax.fori_loop(1, n_dev, err_drain, 0)
 
 
-def grad_kernel(a_ref, b_ref, stat_ref, gq_ref, got_ref):
+def grad_kernel(a_ref, b_ref, stat_ref, gq_hbm, got_hbm, fit_ref, gq_ref, got_ref, sem):
     pack_a = a_ref[...]
     pack_b = b_ref[...].astype(f32)
-    rows = pack_a.shape[0]
+    rows, cols = pack_b.shape
     row = lax.broadcasted_iota(jnp.int32, (rows, 128), 0)
     lane = lax.broadcasted_iota(jnp.int32, (rows, 128), 1)
     per_row = jnp.sum(jnp.where(lane == row // PACK, stat_ref[1:2, :], 0.0), axis=1, keepdims=True)
     per_row = per_row / (noise_scale * noise_scale)
     kind = lax.rem(lax.broadcasted_iota(jnp.int32, (rows, 1), 0), PACK)
-    for out, weight in (
-        (gq_ref, jnp.where(kind < RANK, per_row, 0.0)),
-        (got_ref, jnp.where(kind >= RANK, per_row, 0.0)),
+    edges = (0, (cols // 2 + 127) // 128 * 128, cols)
+    copies = []
+    for out, target, weight in (
+        (gq_ref, gq_hbm, jnp.where(kind < RANK, per_row, 0.0)),
+        (got_ref, got_hbm, jnp.where(kind >= RANK, per_row, 0.0)),
     ):
-        out[...] = sum(dot(s, pack_a, ((0,), (0,))) for s in split3(pack_b * weight))
+        pieces = jnp.concatenate(split3(pack_b * weight), axis=0)
+        right = jnp.concatenate([pack_a] * 3, axis=0)
+        for low, high in zip(edges[:-1], edges[1:]):
+            out[low:high, :] = dot(pieces[:, low:high], right, ((0,), (0,)))
+            copy = pltpu.make_async_copy(
+                out.at[low:high], target.at[low:high], sem.at[len(copies)]
+            )
+            copy.start()
+            copies.append(copy)
+    me = lax.axis_index("pop")
+    fit_ref[0] = jnp.sum(jnp.where(lane[:1] == me, stat_ref[0:1, :], 0.0))
+    for copy in copies:
+        copy.wait()
 
 
 def per_device_fast(
@@ -392,7 +437,6 @@
     cols = w_out.shape[1]
     own_tok = tok // n_pop
     rows = n_pop * own_tok
-    me = lax.axis_index("pop")
     cosine, sine = rope_tables(tok, HEAD_DIM)
     vmem = pl.BlockSpec(memory_space=pltpu.VMEM)
     hbm = pl.BlockSpec(memory_space=pltpu.HBM)
@@ -415,12 +459,16 @@
         out_specs=(vmem, vmem, vmem),
         scratch_shapes=[
             like(tokens), like(w_query), like(w_key), like(w_value), like(wot), like(target),
-            pltpu.VMEM((n_pop, own_tok, feats), LINK),
-            pltpu.VMEM((n_pop, own_tok, feats), LINK),
-            pltpu.VMEM((n_pop, own_tok, 128), bf16),
-            pltpu.VMEM((n_pop, own_tok, 128), bf16),
-            pltpu.VMEM((PACK, feats), bf16),
-            pltpu.VMEM((n_pop, PACK, feats), bf16),
+            pltpu.VMEM((n_pop, own_tok, cut), LINK),
+            pltpu.VMEM((n_pop, own_tok, feats - cut), LINK),
+            pltpu.VMEM((n_pop, own_tok, cut), LINK),
+            pltpu.VMEM((n_pop, own_tok, feats - cut), LINK),
+            pltpu.VMEM((n_pop, RANK, 128), bf16),
+            pltpu.VMEM((n_pop, RANK, 128), bf16),
+            pltpu.VMEM((RANK, feats), bf16),
+            pltpu.VMEM((n_pop, RANK, feats), bf16),
+            pltpu.VMEM((RANK, feats), bf16),
+            pltpu.VMEM((n_pop, RANK, feats), bf16),
             pltpu.VMEM((n_pop, PACK, cols), bf16),
             pltpu.VMEM((n_pop, PACK, cols), bf16),
             pltpu.VMEM((n_pop, rows, cut), bf16),
@@ -431,8 +479,7 @@
             pltpu.VMEM((tok, cols), bf16),
             pltpu.VMEM((n_dev, 1, 128), f32),
             dma((6,)),
-            dma((n_pop,)), dma((n_pop,)), dma((n_pop,)), dma((n_pop,)),
-            dma((n_pop,)), dma((n_pop,)), dma((n_pop,)), dma((n_pop,)),
+            dma((6, n_pop)), dma((6, n_pop)),
             dma((2, depth, 2)), dma((2, depth, 2)),
             dma((n_pop, n_mp)), dma((n_mp, n_pop)),
             dma((n_mp,)), dma,
@@ -444,17 +491,15 @@
     )(tokens, w_query, w_key, w_value, wot, target,
       query_left_factors[0].T, query_right_factors[0], o_left[0].T, o_right[0], member_ids,
       jnp.asarray(cosine), jnp.asarray(sine))
-    grad_query, grad_out_t = pl.pallas_call(
+    grad = jax.ShapeDtypeStruct((cols, feats), f32)
+    grad_query, grad_out_t, fitness = pl.pallas_call(
         grad_kernel,
         name="grads",
-        out_shape=(
-            jax.ShapeDtypeStruct((cols, feats), f32),
-            jax.ShapeDtypeStruct((cols, feats), f32),
-        ),
+        out_shape=(grad, grad, jax.ShapeDtypeStruct((1,), f32)),
         in_specs=[vmem, vmem, vmem],
-        out_specs=(vmem, vmem),
+        out_specs=(hbm, hbm, smem),
+        scratch_shapes=[like(grad), like(grad), dma((4,))],
     )(pack_a, pack_b, stat)
-    fitness = lax.dynamic_slice(stat[0], (me,), (1,))
     return grad_query, grad_out_t.T, fitness
 
 
@@ -588,6 +633,7 @@
         and n_pop % 2 == 0
         and n_pop * PACK <= 128
         and tok % (n_pop * 16) == 0
+        and tok // n_pop < 128
         and args[2].shape[1] // n_mp == 2 * args[5].shape[1] // n_pop
         and args[2].shape[0] == args[5].shape[1]
         and args[3].shape[1] == n_mp * HEAD_DIM

time: 82.6 us -> 76.3 us (0.924)
  Pallas kernels: 79.8 us -> 74.8 us
  local copies, waits for them, and re-layouts: 1.26 us -> 0 us
    pallas_call x1, Pallas kernels: 76 us -> 71.2 us  [per_device_fast(): pl.pallas_call(functools.partial(forward_kernel, n_pop, n_mp, width), nam...]
where the time goes in v3:
time: 76.3 us; the launch traced here: 76.1 us
  Pallas kernels  74.8 us (98%)
  between operations  1.29 us (2%)
    pallas_call x1, Pallas kernels, per_device_fast(): pl.pallas_call(functools.partial(forward_kernel, n_pop, n_mp, width), nam...  71.2 us
    pallas_call x1, Pallas kernels, per_device_fast(): pl.pallas_call(grad_kernel, name='grads', out_shape=(grad, grad, jax.Shap...  3.6 us

profile of v3, /device:TPU:0, one launch (start us, length us, event | category | flops | bytes accessed | tf_op | source)
XLA Modules:
  0.0 76.1 jit_solution(7999476859627990513)
XLA Ops:
  1.3 71.2 %forward.1 = (bf16[64,896]{1,0:T(8,128)(2,1)}, bf16[64,448]{1,0:T(8,128)(2,1)}, f32[8,128]{1,0:T(8,128)}) custom-call(bf16[256,3584]{1,0:T(8,128)(2,1)} %tok_hbm.1, bf16[448,896]{1,0:T(8,128)(2,1)} %wq_hbm.1, bf16[3584,128]{1,0:T(8,128)(2,1)} %wk_hbm.1, bf16[3584,128]{1,0:T(8,128)(2,1)} %wv_hbm.1, bf16[448,896]{1,0:T(8,128)(2,1)} %bitcast.10, ...), custom_call_target="tpu_custom_call" | custom-call | tf_op jit(solution)/shard_map/forward/pallas_call | solution.py:450
  72.5 3.6 %grads.1 = (f32[448,896]{1,0:T(8,128)}, f32[448,896]{1,0:T(8,128)}, f32[1]{0:T(128)}) custom-call(bf16[64,896]{1,0:T(8,128)(2,1)} %get-tuple-element.9.a_ref, bf16[64,448]{1,0:T(8,128)(2,1)} %get-tuple-element.10.b_ref, f32[8,128]{1,0:T(8,128)} %get-tuple-element.11.stat_ref), custom_call_target="tpu_custom_call" | custom-call | tf_op jit(solution)/shard_map/grads/pallas_call | solution.py:495

commit v4 on v3

--- a/solution.py
+++ b/solution.py
@@ -33,6 +33,11 @@
     )
 
 
+def head_groups(feats):
+    heads = feats // HEAD_DIM
+    return [(h * HEAD_DIM, min(h + 2, heads) * HEAD_DIM) for h in range(0, heads, 2)]
+
+
 def dot(a, b, dims=((1,), (0,))):
     return lax.dot_general(a, b, (dims, ((), ())), preferred_element_type=f32)
 
@@ -50,18 +55,22 @@
     tok_hbm, wq_hbm, wk_hbm, wv_hbm, wo_hbm, tgt_hbm, ql_ref, qr_ref, ol_ref, or_ref, id_ref,
     cos_ref, sin_ref,
     pack_a_out, pack_b_out, stat_out,
-    tok_ref, wq_ref, wk_ref, wv_ref, wo_ref, tgt_ref,
-    part_a, part_b, parts_a, parts_b, mine_l, packs_l, mine_q, packs_q, mine_o, packs_o,
-    mine_b, packs_b, ring_a, ring_b,
-    terms, terms_in, tgt_own, target, errs, load_sem,
-    pop_send, pop_recv,
-    ring_send, ring_recv, term_send, term_recv, tgt_send, tgt_recv, err_send, err_recv,
+    *refs,
 ):
+    groups = head_groups(wq_hbm.shape[1])
+    many = len(groups)
+    tok_ref, window_ref, wq_ref, wkv_ref, wo_ref, tgt_ref = refs[:6]
+    refs = refs[6:]
+    mine_base, base_in, rings = refs[:many], refs[many:2 * many], refs[2 * many:3 * many]
+    (
+        mine_l, packs_l, mine_q, packs_q, mine_o, packs_o, mine_b, packs_b,
+        terms, terms_in, tgt_own, target, errs, load_sem, pop_send, pop_recv,
+        ring_send, ring_recv, term_send, term_recv, tgt_send, tgt_recv, err_send, err_recv,
+    ) = refs[3 * many:]
     me = lax.axis_index("pop")
     mc = lax.axis_index("mp")
     n_dev = n_pop * n_mp
     tok, feats = tok_ref.shape[0], wq_ref.shape[1]
-    cut = ring_a.shape[2]
     own_tok = tok // n_pop
     rows = n_pop * own_tok
     per_mp = rows // n_mp
@@ -70,10 +79,13 @@
     members = n_pop // n_mp
     odd = lax.rem(me, 2) == 1
 
+    kv_dim = wk_hbm.shape[1]
+    around = pl.ds(pl.multiple_of(me // 2 * 2 * cols, 128), 2 * cols)
     loads = [
         pltpu.make_async_copy(src, dst, load_sem.at[i])
         for i, (src, dst) in enumerate((
-            (tok_hbm, tok_ref), (wq_hbm, wq_ref), (wk_hbm, wk_ref), (wv_hbm, wv_ref),
+            (wq_hbm, wq_ref), (tok_hbm.at[:, around], window_ref), (tok_hbm, tok_ref),
+            (wk_hbm, wkv_ref.at[:, :kv_dim]), (wv_hbm, wkv_ref.at[:, kv_dim:]),
             (tgt_hbm, tgt_ref), (wo_hbm, wo_ref),
         ))
     ]
@@ -97,12 +109,12 @@
     factor = noise_scale * sign.astype(f32)
     loads[0].wait()
     loads[1].wait()
-    window = tok_ref[:, pl.ds(pl.multiple_of(me // 2 * 2 * cols, 128), 2 * cols)]
+    window = window_ref[...]
     wq = wq_ref[...]
     first, second = window[:, :cols], window[:, cols:]
     base = dot(jnp.where(odd, second, first), wq)
-    part_a[...] = base[:, :cut].reshape(part_a.shape).astype(LINK)
-    part_b[...] = base[:, cut:].reshape(part_b.shape).astype(LINK)
+    for mine, (low, high) in zip(mine_base, groups):
+        mine[...] = base[:, low:high].reshape(mine.shape).astype(LINK)
     mine_q[...] = (qr_ref[...].astype(f32) * factor).astype(bf16)
 
     pl.semaphore_wait(barrier, n_dev - 1)
@@ -110,12 +122,11 @@
     def to_pop(i, kind):
         other = lax.rem(me + i, n_pop)
         src, dst = (
-            (part_a.at[other], parts_a),
             (mine_q, packs_q),
             (mine_l.at[other], packs_l),
-            (part_b.at[other], parts_b),
             (mine_o, packs_o),
             (mine_b.at[other], packs_b),
+            *((mine.at[other], landing) for mine, landing in zip(mine_base, base_in)),
         )[kind]
         return pltpu.make_async_remote_copy(
             src_ref=src, dst_ref=dst.at[me], send_sem=pop_send.at[kind, i],
@@ -130,23 +141,25 @@
         for i in range(1, n_pop):
             to_pop(i, kind).wait_recv()
 
+    to_all(4)
     to_all(0)
-    to_all(1)
+    loads[2].wait()
     ql = ql_ref[...]
     low = dot(ql, tok_ref[...], ((1,), (1,))).astype(bf16).astype(f32)
     for q in range(n_pop):
         mine_l[q] = jnp.concatenate(
             [low[:, q * own_tok:(q + 1) * own_tok], jnp.zeros((RANK, 128 - own_tok), f32)], axis=1
         ).astype(bf16)
-    to_all(2)
-    to_all(3)
+    to_all(1)
+    for g in range(1, many):
+        to_all(4 + g)
     mine_o[...] = ol_ref[...]
     both = jnp.concatenate([ql.astype(f32), or_ref[...].astype(f32) * factor], axis=0)
     for q in range(n_pop):
         mine_b[q] = both[:, q * cols:(q + 1) * cols].astype(bf16)
-    to_all(4)
-    to_all(5)
-    for mine, packs in ((part_a, parts_a), (part_b, parts_b), (mine_l, packs_l), (mine_b, packs_b)):
+    to_all(2)
+    to_all(3)
+    for mine, packs in (*zip(mine_base, base_in), (mine_l, packs_l), (mine_b, packs_b)):
         packs[me] = mine[me]
     packs_q[me] = mine_q[...]
     packs_o[me] = mine_o[...]
@@ -159,7 +172,7 @@
             device_id={"mp": lax.rem(mc + i, n_mp)}, device_id_type=MESH,
         )
 
-    loads[4].wait()
+    loads[5].wait()
 
     @pl.when(mc == owner)
     def _():
@@ -168,12 +181,13 @@
             target_copy(i).start()
         target[...] = tgt_own[...]
 
-    loads[2].wait()
     loads[3].wait()
+    loads[4].wait()
     cosine, sine = cos_ref[...], sin_ref[...]
-    key = dot(tok_ref[...], wk_ref[...])
+    kv = dot(tok_ref[...], wkv_ref[...])
+    key = kv[:, :kv_dim]
     key = (key * cosine + pltpu.roll(key, HEAD_DIM // 2, 1) * sine).astype(bf16)
-    value = dot(tok_ref[...], wv_ref[...]).astype(bf16)
+    value = kv[:, kv_dim:].astype(bf16)
 
     start = pl.multiple_of(me * own_tok, own_tok)
     cos_own = jnp.tile(cos_ref[pl.ds(start, own_tok), :], (n_pop, 1))
@@ -182,8 +196,8 @@
     causal = token_of >= lax.broadcasted_iota(jnp.int32, (rows, tok), 1)
     scale = HEAD_DIM ** (-0.5)
 
-    for kind in range(3):
-        from_all(kind)
+    from_all(0)
+    from_all(1)
 
     def pop_at(r):
         r = lax.rem(r + 2 * n_pop, n_pop)
@@ -193,7 +207,6 @@
     right, left = pop_at(my_r + 1), pop_at(my_r - 1)
 
     depth = n_pop // 2
-    rings = (ring_a, ring_b)
 
     def hop(direction, step, g):
         at = pop_at(my_r - step if direction == 0 else my_r + step)
@@ -204,7 +217,7 @@
         )
 
     def hops(direction, step, g):
-        return step < depth - 1 or (step == depth - 1 and g == direction)
+        return step < depth - 1 or (step == depth - 1 and (2 * g >= many) == (direction == 1))
 
     def stacked(parts, *more):
         return jnp.concatenate(
@@ -222,15 +235,13 @@
     of_rank = lax.broadcasted_iota(jnp.int32, low_rows.shape, 1) // RANK
     of_row = lax.broadcasted_iota(jnp.int32, low_rows.shape, 0) // own_tok
     low_rows = jnp.where(of_rank == of_row, low_rows, 0.0).astype(bf16)
-    group = ring_a.shape[2] // HEAD_DIM
     for h in range(heads):
         lanes = slice(h * HEAD_DIM, (h + 1) * HEAD_DIM)
-        g = 0 if h < group else 1
-        at = h - g * group
-        here = slice(at * HEAD_DIM, (at + 1) * HEAD_DIM)
-        if h == group:
-            from_all(3)
-        parts = (parts_a, parts_b)[g]
+        g = [low <= lanes.start < high for low, high in groups].index(True)
+        here = slice(lanes.start - groups[g][0], lanes.stop - groups[g][0])
+        if here.start == 0:
+            from_all(4 + g)
+        parts = base_in[g]
         total = parts[0, :, here].astype(f32)
         for i in range(1, n_pop):
             total = total + parts[i, :, here].astype(f32)
@@ -242,17 +253,17 @@
         prob = (e / jnp.sum(e, axis=1, keepdims=True)).astype(bf16)
         mixed = dot(prob, value).astype(bf16)
         rings[g][me, :, here] = mixed
-        if h in (group - 1, heads - 1):
+        if lanes.stop == groups[g][1]:
             for direction in range(2):
                 hop(direction, 0, g).start()
 
-    from_all(4)
-    from_all(5)
+    from_all(2)
+    from_all(3)
     pack_a = stacked(packs_q, packs_o)
     pack_b = stacked(packs_b)
     pack_a_out[...] = pack_a
     pack_b_out[...] = pack_b
-    loads[5].wait()
+    loads[6].wait()
 
     def term_copy(at, block):
         return pltpu.make_async_remote_copy(
@@ -267,11 +278,12 @@
     keep = (place // PACK == member_of) & (lax.rem(place, PACK) >= RANK)
 
     def project(at):
-        xa, xb = ring_a[at], ring_b[at]
         nt = ((1,), (1,))
-        low = dot(xa, pack_a[:, :cut], nt) + dot(xb, pack_a[:, cut:], nt)
+        low = sum(
+            dot(ring[at], pack_a[:, a:b], nt) for ring, (a, b) in zip(rings, groups)
+        )
         low = jnp.where(keep, low, 0.0)
-        y = dot(xa, wo_ref[:, :cut], nt) + dot(xb, wo_ref[:, cut:], nt)
+        y = sum(dot(ring[at], wo_ref[:, a:b], nt) for ring, (a, b) in zip(rings, groups))
         for piece in split3(low):
             y = y + dot(piece, pack_b)
         y = y.astype(bf16)
@@ -314,7 +326,7 @@
     totals = [jnp.zeros((1, cols), f32)] * members
     done = [me]
     for step in range(depth):
-        for g in range(2):
+        for g in range(many):
             for direction in range(2):
                 if hops(direction, step, g):
                     hop(direction, step, g).wait_recv()
@@ -357,11 +369,11 @@
         return carry
 
     lax.fori_loop(1, n_dev, err_start, 0)
-    for kind in range(6):
+    for kind in range(4 + many):
         for i in range(1, n_pop):
             to_pop(i, kind).wait_send()
     for step in range(depth):
-        for g in range(2):
+        for g in range(many):
             for direction in range(2):
                 if hops(direction, step, g):
                     hop(direction, step, g).wait_send()
@@ -444,7 +456,7 @@
     dma = pltpu.SemaphoreType.DMA
     depth = n_pop // 2
     n_dev = n_pop * n_mp
-    cut = (feats // HEAD_DIM + 1) // 2 * HEAD_DIM
+    widths = [high - low for low, high in head_groups(feats)]
     like = lambda x: pltpu.VMEM(x.shape, x.dtype)
     wot = w_out.T
     pack_a, pack_b, stat = pl.pallas_call(
@@ -458,11 +470,11 @@
         in_specs=[hbm] * 6 + [vmem] * 4 + [smem] + [vmem] * 2,
         out_specs=(vmem, vmem, vmem),
         scratch_shapes=[
-            like(tokens), like(w_query), like(w_key), like(w_value), like(wot), like(target),
-            pltpu.VMEM((n_pop, own_tok, cut), LINK),
-            pltpu.VMEM((n_pop, own_tok, feats - cut), LINK),
-            pltpu.VMEM((n_pop, own_tok, cut), LINK),
-            pltpu.VMEM((n_pop, own_tok, feats - cut), LINK),
+            like(tokens), pltpu.VMEM((tok, 2 * cols), bf16), like(w_query),
+            pltpu.VMEM((w_key.shape[0], 2 * w_key.shape[1]), bf16), like(wot), like(target),
+            *(pltpu.VMEM((n_pop, own_tok, w), LINK) for w in widths),
+            *(pltpu.VMEM((n_pop, own_tok, w), LINK) for w in widths),
+            *(pltpu.VMEM((n_pop, rows, w), bf16) for w in widths),
             pltpu.VMEM((n_pop, RANK, 128), bf16),
             pltpu.VMEM((n_pop, RANK, 128), bf16),
             pltpu.VMEM((RANK, feats), bf16),
@@ -471,16 +483,14 @@
             pltpu.VMEM((n_pop, RANK, feats), bf16),
             pltpu.VMEM((n_pop, PACK, cols), bf16),
             pltpu.VMEM((n_pop, PACK, cols), bf16),
-            pltpu.VMEM((n_pop, rows, cut), bf16),
-            pltpu.VMEM((n_pop, rows, feats - cut), bf16),
             pltpu.VMEM((n_pop, n_mp, rows // n_mp, cols), bf16),
             pltpu.VMEM((n_mp, n_pop, rows // n_mp, cols), bf16),
             pltpu.VMEM((tok, cols), bf16),
             pltpu.VMEM((tok, cols), bf16),
             pltpu.VMEM((n_dev, 1, 128), f32),
-            dma((6,)),
-            dma((6, n_pop)), dma((6, n_pop)),
-            dma((2, depth, 2)), dma((2, depth, 2)),
+            dma((7,)),
+            dma((4 + len(widths), n_pop)), dma((4 + len(widths), n_pop)),
+            dma((2, depth, len(widths))), dma((2, depth, len(widths))),
             dma((n_pop, n_mp)), dma((n_mp, n_pop)),
             dma((n_mp,)), dma,
             dma((n_dev,)), dma((n_dev,)),

time: 76.3 us -> 76.8 us (level)
  no operation moved by 1% of the time
where the time goes in v4:
time: 76.8 us; the launch traced here: 76.6 us
  Pallas kernels  75.3 us (98%)
  between operations  1.29 us (2%)
    pallas_call x1, Pallas kernels, per_device_fast(): pl.pallas_call(functools.partial(forward_kernel, n_pop, n_mp, width), nam...  71.7 us
    pallas_call x1, Pallas kernels, per_device_fast(): pl.pallas_call(grad_kernel, name='grads', out_shape=(grad, grad, jax.Shap...  3.6 us

profile of v4, /device:TPU:0, one launch (start us, length us, event | category | flops | bytes accessed | tf_op | source)
XLA Modules:
  0.0 76.6 jit_solution(9659852972539872659)
XLA Ops:
  1.3 71.7 %forward.1 = (bf16[64,896]{1,0:T(8,128)(2,1)}, bf16[64,448]{1,0:T(8,128)(2,1)}, f32[8,128]{1,0:T(8,128)}) custom-call(bf16[256,3584]{1,0:T(8,128)(2,1)} %tok_hbm.1, bf16[448,896]{1,0:T(8,128)(2,1)} %wq_hbm.1, bf16[3584,128]{1,0:T(8,128)(2,1)} %wk_hbm.1, bf16[3584,128]{1,0:T(8,128)(2,1)} %wv_hbm.1, bf16[448,896]{1,0:T(8,128)(2,1)} %bitcast.10, ...), custom_call_target="tpu_custom_call" | custom-call | tf_op jit(solution)/shard_map/forward/pallas_call | solution.py:462
  73.0 3.6 %grads.1 = (f32[448,896]{1,0:T(8,128)}, f32[448,896]{1,0:T(8,128)}, f32[1]{0:T(128)}) custom-call(bf16[64,896]{1,0:T(8,128)(2,1)} %get-tuple-element.9.a_ref, bf16[64,448]{1,0:T(8,128)(2,1)} %get-tuple-element.10.b_ref, f32[8,128]{1,0:T(8,128)} %get-tuple-element.11.stat_ref), custom_call_target="tpu_custom_call" | custom-call | tf_op jit(solution)/shard_map/grads/pallas_call | solution.py:505

commit v5 on v4

--- a/solution.py
+++ b/solution.py
@@ -35,7 +35,7 @@
 
 def head_groups(feats):
     heads = feats // HEAD_DIM
-    return [(h * HEAD_DIM, min(h + 2, heads) * HEAD_DIM) for h in range(0, heads, 2)]
+    return [(h * HEAD_DIM, min(h + 4, heads) * HEAD_DIM) for h in range(0, heads, 4)]
 
 
 def dot(a, b, dims=((1,), (0,))):

time: 76.8 us -> 76.3 us (level)
  no operation moved by 1% of the time
where the time goes in v5:
time: 76.3 us; the launch traced here: 76.1 us
  Pallas kernels  74.9 us (98%)
  between operations  1.29 us (2%)
    pallas_call x1, Pallas kernels, per_device_fast(): pl.pallas_call(functools.partial(forward_kernel, n_pop, n_mp, width), nam...  71.2 us
    pallas_call x1, Pallas kernels, per_device_fast(): pl.pallas_call(grad_kernel, name='grads', out_shape=(grad, grad, jax.Shap...  3.6 us

profile of v5, /device:TPU:0, one launch (start us, length us, event | category | flops | bytes accessed | tf_op | source)
XLA Modules:
  0.0 76.1 jit_solution(2398105707894759185)
XLA Ops:
  1.3 71.2 %forward.1 = (bf16[64,896]{1,0:T(8,128)(2,1)}, bf16[64,448]{1,0:T(8,128)(2,1)}, f32[8,128]{1,0:T(8,128)}) custom-call(bf16[256,3584]{1,0:T(8,128)(2,1)} %tok_hbm.1, bf16[448,896]{1,0:T(8,128)(2,1)} %wq_hbm.1, bf16[3584,128]{1,0:T(8,128)(2,1)} %wk_hbm.1, bf16[3584,128]{1,0:T(8,128)(2,1)} %wv_hbm.1, bf16[448,896]{1,0:T(8,128)(2,1)} %bitcast.10, ...), custom_call_target="tpu_custom_call" | custom-call | tf_op jit(solution)/shard_map/forward/pallas_call | solution.py:462
  72.5 3.6 %grads.1 = (f32[448,896]{1,0:T(8,128)}, f32[448,896]{1,0:T(8,128)}, f32[1]{0:T(128)}) custom-call(bf16[64,896]{1,0:T(8,128)(2,1)} %get-tuple-element.9.a_ref, bf16[64,448]{1,0:T(8,128)(2,1)} %get-tuple-element.10.b_ref, f32[8,128]{1,0:T(8,128)} %get-tuple-element.11.stat_ref), custom_call_target="tpu_custom_call" | custom-call | tf_op jit(solution)/shard_map/grads/pallas_call | solution.py:505
